TPU v7x, 32 devices: a whole 2x2x4 slice. The times are simulated.
32 devices in a mesh: lon: 8 (over z, core), colat: 4 (over y, x).
Axes of the slice: x: 2, y: 2, z: 4, core: 2. Of those that a mesh axis runs over, the one named last changes fastest.
Arguments:
- forward_state: float32 [9, 8, 64, 1024], P(None, None, 'colat', 'lon'), may hold values from -6 to 6
- adjoint_state: float32 [9, 8, 64, 1024], P(None, None, 'colat', 'lon'), may hold values from -6 to 6
- layer_ids: int32 [8, 64, 1024], P(None, 'colat', 'lon'), may hold values from 0 to 15
- density_table: float32 [16], replicated, may hold values from 2 to 4
- lame_table: float32 [16], replicated, may hold values from 0.5 to 2
- shear_table: float32 [16], replicated, may hold values from 0.5 to 1.5
- source_cells: int32 [8], replicated, may hold values from 0 to 524287
- source_wavelet: float32 [2, 8], replicated, may hold values from -6 to 6
- receiver_cells: int32 [512], replicated, may hold values from 0 to 524287
- receiver_residual: float32 [2, 3, 512], replicated, may hold values from -6 to 6
Outputs:
- forward_field: float32 [9, 8, 64, 1024], P(None, None, 'colat', 'lon')
- adjoint_field: float32 [9, 8, 64, 1024], P(None, None, 'colat', 'lon')
- density_kernel: float32 [8, 64, 1024], P(None, 'colat', 'lon')
Inputs may be any that keep to these rules, and one draw needn't show every extreme that they name: `source_cells`: flat index (level * 64 + colatitude) * 1024 + longitude. `receiver_cells`: flat index as for the sources.
All inputs are finite; a program needn't handle non-finite values.
Results may differ from a plain program's by a relative error of at most 0.0001.
Values sent between devices are 32-bit elements; how exact they have to be, the bound alone decides.
No kernel may reach another device: no remote copies, remote signals or barrier semaphores. Data moves between devices by JAX's collectives and lax.ppermute only.
A program may use at most 64 MiB of HBM per device.

v0:
```python
import functools
import math

import jax
import jax.numpy as jnp
from jax import lax
from jax.experimental import pallas as pl
from jax.experimental.pallas import tpu as pltpu
from jax.sharding import PartitionSpec as P

R_INNER = 0.55
COURANT = 0.3
SIN_FLOOR = 0.25
FIELD_SIGNS = (-1, -1, 1, 1, 1, 1, 1, -1, -1)
CROSS = (3, 6, 7)
OTHER = (4, 5, 8)
EDGE = 8
LANES = 128
V_ROWS = 6
S_ROWS = 4
F32 = jnp.float32


NEAR = tuple((f, c, d) for f in range(2) for c in CROSS for d in (1, 2))
FAR = tuple((f, c, d) for f in range(2) for c in OTHER for d in (1, 2)) + tuple(
    (f, c, d) for f in range(2) for c in CROSS for d in (3, 4)
)
FAR_IDS = len(FAR)
VEL = tuple((f, c, d) for f in range(2) for c in range(3) for d in range(1, V_ROWS + 1))


def vmem():
    return pl.BlockSpec(memory_space=pltpu.VMEM)


def smem():
    return pl.BlockSpec(memory_space=pltpu.SMEM)


def lane_iota(shape):
    return lax.broadcasted_iota(jnp.int32, shape, 1)


def rolled(x, shift, axis=1):
    size = x.shape[axis]
    shift = shift % size
    return x if shift == 0 else pltpu.roll(x, shift, axis)


class Packer:
    def __init__(self, ref, width, base=0):
        self.ref, self.width, self.base = ref, width, base
        self.per = LANES // width
        self.count, self.value = 0, None

    def add(self, x, start):
        slot = self.count % self.per
        moved = rolled(x, slot * self.width - start)
        if slot == 0:
            self.value = moved
        else:
            self.value = jnp.where(lane_iota(x.shape) >= slot * self.width, moved, self.value)
        self.count += 1
        if self.count % self.per == 0:
            self.flush()

    def flush(self):
        if self.value is not None:
            self.ref[self.base + (self.count - 1) // self.per] = self.value
            self.value = None


def pieces(count, width):
    per = LANES // width
    return -(-count // per)


def halo_vector(east, west, slot):
    after = rolled(east, -slot * EDGE)
    before = rolled(west, LANES - EDGE - slot * EDGE)
    return jnp.where(lane_iota(after.shape) < LANES // 2, after, before)


def even_band():
    return lax.rem(lax.axis_index("colat"), 2) == 0


def even_tile():
    return lax.rem(lax.axis_index("lon"), 2) == 0


def pole_signs():
    band, last = lax.axis_index("colat"), lax.axis_size("colat") - 1
    north = jnp.where(band == 0, -1.0, 1.0).astype(F32)
    south = jnp.where(band == last, -1.0, 1.0).astype(F32)
    return north, south


def strided(ref, first, levels, rows):
    return ref[pl.ds(first, levels, stride=rows), :]


def pack_kernel(dims, state, edge_a, edge_b, near_a, near_b, far_a, far_b):
    levels, rows, cols = dims
    even = even_band()

    def row(f, c, r):
        return strided(state, (f * 9 + c) * levels * rows + r, levels, rows)

    def id_row(r):
        return strided(state, 18 * levels * rows + r, levels, rows)

    def put(ref_a, ref_b, k, get, d):
        top, bottom = get(d - 1), get(rows - d)
        ref_a[k], ref_b[k] = jnp.where(even, bottom, top), jnp.where(even, top, bottom)

    for k, (f, c, d) in enumerate(NEAR):
        put(near_a, near_b, k, functools.partial(row, f, c), d)
    for k, (f, c, d) in enumerate(FAR):
        put(far_a, far_b, k, functools.partial(row, f, c), d)
    for d in range(1, S_ROWS + 1):
        put(far_a, far_b, FAR_IDS + d - 1, id_row, d)

    east, west = Packer(edge_a, EDGE), Packer(edge_b, EDGE)

    def both(x):
        east.add(x[:, cols - LANES :], LANES - EDGE)
        west.add(x[:, :LANES], 0)

    for f in range(2):
        for c in range(9):
            for r in range(rows):
                both(row(f, c, r))
    for r in range(rows):
        both(id_row(r))
    east.flush()
    west.flush()

    @pl.when(jnp.logical_not(even_tile()))
    def _():
        for v in range(edge_a.shape[0]):
            edge_a[v], edge_b[v] = edge_b[v], edge_a[v]


def divided(x, by):
    q = jnp.floor(x.astype(F32) * (1.0 / by)).astype(jnp.int32)
    r = x - q * by
    q = q + jnp.where(r >= by, 1, 0) - jnp.where(r < 0, 1, 0)
    return q, x - q * by


def inject(dims, extents, step, given, out, halo):
    levels, rows, cols = dims
    lat_cells, lon_cells = extents
    width = cols + LANES
    north_sign, south_sign = pole_signs()
    first_row, first_col = lax.axis_index("colat") * rows, lax.axis_index("lon") * cols
    at_top, at_bottom = first_row == 0, first_row + rows == lat_cells
    half = lon_cells // 2

    def located(ids):
        level, rest = divided(ids, lat_cells * lon_cells)
        row, col = divided(rest, lon_cells)

        def lane(c):
            x = c - first_col
            x = jnp.where(x < 0, x + lon_cells, x)
            x = jnp.where(x >= lon_cells, x - lon_cells, x)
            tail = x - lon_cells + cols + LANES
            tail = jnp.where(tail >= cols + LANES - EDGE, tail, -1)
            return jnp.where(x < cols + EDGE, x, tail)

        def code(r, count):
            inside = jnp.logical_and(r >= 0, r < count)
            return jnp.where(inside, r * levels + level, -1)

        north = 1 - jnp.where(at_top, row, first_row - 1 - row)
        south = jnp.where(at_bottom, lat_cells - 1 - row, row - first_row - rows)
        return (
            (code(row - first_row, rows), lane(col)),
            (code(north, 2), lane(jnp.where(at_top, col + half, col))),
            (code(south, 2), lane(jnp.where(at_bottom, col + half, col))),
        )

    def spread(place, value_rows, count):
        code, lane = place
        n = code.shape[1]
        hot_rows = lax.broadcasted_iota(jnp.int32, (count * levels, n), 0) == code
        hot = lax.broadcasted_iota(jnp.int32, (width, n), 0) == lane
        hot = jnp.where(hot, 1.0, 0.0).astype(jnp.bfloat16)
        out = []
        for value in value_rows:
            rest = jnp.where(hot_rows, value, 0.0)
            total = None
            for _ in range(3):
                part = rest.astype(jnp.bfloat16)
                rest = rest - part.astype(F32)
                term = lax.dot_general(
                    part, hot, (((1,), (1,)), ((), ())), preferred_element_type=F32
                )
                total = term if total is None else total + term
            out.append(total.reshape(count, levels, width))
        return out

    places = located(given[0:1, :].astype(jnp.int32))
    splaces = located(given[7:8, :LANES].astype(jnp.int32))
    values = [given[1 + 3 * step + c : 2 + 3 * step + c, :] for c in range(3)]
    svalues = [given[8 + step : 9 + step, :LANES]]
    regions = ((0, halo, rows, 1.0), (1, 0, halo, north_sign), (2, halo + rows, halo, south_sign))
    for where, at, count, sign in regions:
        if count:
            out[0, at : at + count] = spread(splaces[where], svalues, count)[0]
            for c, got in enumerate(spread(places[where], values, count)):
                signed = where and FIELD_SIGNS[c] < 0
                out[1 + c, at : at + count] = got * sign if signed else got


def first_inject_kernel(dims, extents, given, out, ap, cv):
    levels, rows, _ = dims
    lat_cells, lon_cells = extents
    first_row = lax.axis_index("colat") * rows
    inject(dims, extents, 0, given, out, 0)
    deep = rows + 2 * S_ROWS
    g = lax.broadcasted_iota(jnp.int32, (deep, LANES), 0) + (first_row - S_ROWS)
    sign = jnp.where(jnp.logical_or(g < 0, g >= lat_cells), -1.0, 1.0)
    g = jnp.where(g < 0, -1 - g, jnp.where(g >= lat_cells, 2 * lat_cells - 1 - g, g))
    angle = (g.astype(F32) + 0.5) * (math.pi / lat_cells)
    held = jnp.maximum(jnp.sin(angle), SIN_FLOOR)
    across = sign / (held * (24.0 * math.pi / lon_cells))
    cot = sign * jnp.cos(angle) / held
    ir = level_vectors(levels, LANES, (1.0 - R_INNER) / levels, math.pi / lat_cells)[0]
    for i in range(deep):
        ap[i] = ir * across[i : i + 1, :]
        cv[i] = ir * cot[i : i + 1, :]


def second_inject_kernel(dims, extents, given, out):
    inject(dims, extents, 1, given, out, 2)


def level_vectors(levels, width, dr, theta_step):
    k = lax.broadcasted_iota(jnp.int32, (levels, width), 0)
    ir = 1.0 / (R_INNER + (k.astype(F32) + 0.5) * dr)
    up = jnp.where(k < levels - 1, 0.5 / dr, 0.0).astype(F32)
    down = jnp.where(k > 0, 0.5 / dr, 0.0).astype(F32)
    return ir, ir * (8.0 / 12.0 / theta_step), ir * (1.0 / 12.0 / theta_step), up, down


def along_theta(ref, k, i, c1, c2):
    return c1 * (ref[k, i + 1] - ref[k, i - 1]) - c2 * (ref[k, i + 2] - ref[k, i - 2])


def along_phi(x):
    return 8.0 * (rolled(x, -1) - rolled(x, 1)) - (rolled(x, -2) - rolled(x, 2))


def along_r(x, up, down):
    return up * rolled(x, -1, 0) - down * rolled(x, 1, 0)


def forces(stress, f, i, vectors, ap, cv):
    ir, c1, c2, up, down = vectors
    k = f * 6
    tt, pp, rr, tp, tr, pr = (stress[k + n, i] for n in range(6))
    f_t = (
        along_theta(stress, k, i, c1, c2)
        + ap * along_phi(tp)
        + along_r(tr, up, down)
        + cv * (tt - pp)
        + 3.0 * (ir * tr)
    )
    f_p = (
        along_theta(stress, k + 3, i, c1, c2)
        + ap * along_phi(pp)
        + along_r(pr, up, down)
        + 2.0 * (cv * tp)
        + 3.0 * (ir * pr)
    )
    f_r = (
        along_theta(stress, k + 4, i, c1, c2)
        + ap * along_phi(pr)
        + along_r(rr, up, down)
        + ir * (2.0 * rr - tt - pp)
        + cv * tr
    )
    return f_t, f_p, f_r


def stress_steps(vel, f, i, vectors, ap, cv, lam, mu2, keep):
    ir, c1, c2, up, down = (v[:, :keep] for v in vectors)
    k = f * 3
    whole = tuple(vel[k + n, i] for n in range(3))
    v_t, v_p, v_r = (x[:, :keep] for x in whole)
    p_t, p_p, p_r = (along_phi(x)[:, :keep] for x in whole)

    def theta(n):
        return c1 * (vel[k + n, i + 1, :, :keep] - vel[k + n, i - 1, :, :keep]) - c2 * (
            vel[k + n, i + 2, :, :keep] - vel[k + n, i - 2, :, :keep]
        )

    ir_r = ir * v_r
    e_tt = theta(0) + ir_r
    e_pp = ap * p_p + cv * v_t + ir_r
    e_rr = along_r(v_r, up, down)
    e_tp = theta(1) - cv * v_p + ap * p_t
    e_tr = along_r(v_t, up, down) - ir * v_t + theta(2)
    e_pr = along_r(v_p, up, down) - ir * v_p + ap * p_r
    bulk = lam * (e_tt + e_pp + e_rr)
    half_mu = 0.5 * mu2
    return (
        bulk + mu2 * e_tt,
        bulk + mu2 * e_pp,
        bulk + mu2 * e_rr,
        half_mu * e_tp,
        half_mu * e_tr,
        half_mu * e_pr,
    )


def look_up(ids, tables):
    out = [jnp.full(ids.shape, table[0], F32) for table in tables]
    for n in range(1, tables[0].shape[0]):
        hit = ids == float(n)
        out = [jnp.where(hit, table[n], x) for table, x in zip(tables, out)]
    return out


def materials(ids, dt, tables):
    rho, lam, mu = look_up(ids, tables)
    return dt / rho, dt * lam, (2.0 * dt) * mu


def widened(x, width):
    return jnp.concatenate([x] * (width // LANES), axis=1)


def north_south(ref_a, ref_b, k):
    even = even_band()
    a, b = ref_a[k], ref_b[k]
    return jnp.where(even, b, a), jnp.where(even, a, b)


def velocity_kernel(
    dims, consts, state, edge_a, edge_b, near_a, near_b, ap, cv, first, density,
    stress, vel, pay_a, pay_b, rho, id_side,
):
    levels, rows, cols = dims
    dr, theta_step, dt = consts
    width = cols + LANES
    signs = pole_signs()
    even = even_band()
    per = LANES // EDGE
    east_first = even_tile()

    def side_of(j):
        a, b = edge_a[j // per], edge_b[j // per]
        return halo_vector(jnp.where(east_first, a, b), jnp.where(east_first, b, a), j % per)

    for f in range(2):
        for c in range(9):
            for r in range(rows):
                main = strided(state, (f * 9 + c) * levels * rows + r, levels, rows)
                side = side_of((f * 9 + c) * rows + r)
                if c < 3:
                    ref, k, i = vel, f * 3 + c, r
                else:
                    ref, k, i = stress, f * 6 + c - 3, r + S_ROWS
                ref[k, i, :, :cols] = main
                ref[k, i, :, cols:] = side
    for r in range(rows):
        main = strided(state, 18 * levels * rows + r, levels, rows)
        side = side_of(18 * rows + r)
        id_side[r] = side
        rho[r, :, :cols] = dt / look_up(main, (density,))[0]
        rho[r, :, cols:] = dt / look_up(side, (density,))[0]
    for k, (f, c, d) in enumerate(NEAR):
        for main, i, sign in zip(
            north_south(near_a, near_b, k), (S_ROWS - d, S_ROWS + rows - 1 + d), signs
        ):
            if FIELD_SIGNS[c] < 0:
                main = main * sign
            stress[f * 6 + c - 3, i, :, :cols] = main
            stress[f * 6 + c - 3, i, :, cols:] = jnp.zeros((levels, LANES), F32)

    vectors = level_vectors(levels, width, dr, theta_step)

    def step(r, carry):
        i = r + S_ROWS
        scale = rho[r]
        row_ap, row_cv = widened(ap[i], width), widened(cv[i], width)
        for f in range(2):
            for c, force in enumerate(forces(stress, f, i, vectors, row_ap, row_cv)):
                new = vel[f * 3 + c, r] + scale * force
                if f == 1 or c == 2:
                    new = new + first[f * (1 + c), r]
                vel[f * 3 + c, r] = new
        return carry

    lax.fori_loop(0, rows, step, 0, unroll=2)

    tiles = cols // LANES
    for ref, bottom_side in ((pay_a, even), (pay_b, jnp.logical_not(even))):
        packer = Packer(ref, 2 * EDGE, len(VEL) * tiles)

        def facing(d):
            return jnp.where(bottom_side, rows - d, d - 1)

        for k, (f, c, d) in enumerate(VEL):
            x = vel[f * 3 + c, facing(d)]
            for t in range(tiles):
                ref[k * tiles + t] = x[:, t * LANES : (t + 1) * LANES]
            packer.add(x[:, cols:], LANES - EDGE)
        for f, c, d in NEAR + FAR:
            packer.add(stress[f * 6 + c - 3, facing(d) + S_ROWS, :, cols:], LANES - EDGE)
        for d in range(1, S_ROWS + 1):
            packer.add(id_side[facing(d)], LANES - EDGE)
        packer.flush()


def fill_kernel(
    dims, dt, stress, state, id_edge_a, id_edge_b, far_a, far_b, density, lame, shear,
    halo, mats,
):
    levels, rows, cols = dims
    signs = pole_signs()
    tables = density, lame, shear
    per = LANES // EDGE
    east_first = even_tile()

    for k, (f, c, d) in enumerate(FAR):
        for main, i, sign in zip(
            north_south(far_a, far_b, k), (S_ROWS - d, S_ROWS - 1 + d), signs
        ):
            halo[f * 6 + c - 3, i] = main * sign if FIELD_SIGNS[c] < 0 else main
    for f, c, d in NEAR:
        k = f * 6 + c - 3
        halo[k, S_ROWS - d] = stress[k, S_ROWS - d, :, :cols]
        halo[k, S_ROWS - 1 + d] = stress[k, S_ROWS + rows - 1 + d, :, :cols]

    def material(i, x, at):
        for n, value in enumerate(materials(x, dt, tables)):
            mats[n, i, :, at] = value

    main, side = slice(0, cols), slice(cols, cols + LANES)
    for r in range(rows):
        material(r + S_ROWS, strided(state, 18 * levels * rows + r, levels, rows), main)
        j = 18 * rows + r
        a, b = id_edge_a[j // per], id_edge_b[j // per]
        x = halo_vector(jnp.where(east_first, a, b), jnp.where(east_first, b, a), j % per)
        material(r + S_ROWS, x, side)
    for d in range(1, S_ROWS + 1):
        north, south = north_south(far_a, far_b, FAR_IDS + d - 1)
        material(S_ROWS - d, north, main)
        material(S_ROWS + rows - 1 + d, south, main)


def final_kernel(
    dims, consts, vel_in, stress_in, halo, got_a, got_b, mats_in, second, ap, cv,
    density_t, lame_t, shear_t, fwd, adj, density, vel, stress, mats,
):
    levels, rows, cols = dims
    dr, theta_step, dt = consts
    width = cols + LANES
    signs = pole_signs()
    tiles = cols // LANES
    per = LANES // (2 * EDGE)
    even = even_band()
    side_at = slice(cols, width)

    def sides(j):
        v = len(VEL) * tiles + j // per
        return (
            rolled(x, -EDGE - (j % per) * 2 * EDGE) for x in north_south(got_a, got_b, v)
        )

    for k, (f, c, d) in enumerate(VEL):
        flip = FIELD_SIGNS[c] < 0
        for t in range(tiles):
            at = slice(t * LANES, (t + 1) * LANES)
            north, south = north_south(got_a, got_b, k * tiles + t)
            vel[f * 3 + c, V_ROWS - d, :, at] = north * signs[0] if flip else north
            vel[f * 3 + c, V_ROWS + rows - 1 + d, :, at] = south * signs[1] if flip else south
        for x, i, sign in zip(sides(k), (V_ROWS - d, V_ROWS + rows - 1 + d), signs):
            vel[f * 3 + c, i, :, side_at] = x * sign if flip else x
    for k, (f, c, d) in enumerate(NEAR + FAR):
        n = f * 6 + c - 3
        for x, i, i_main, sign in zip(
            sides(len(VEL) + k),
            (S_ROWS - d, S_ROWS + rows - 1 + d),
            (S_ROWS - d, S_ROWS - 1 + d),
            signs,
        ):
            stress[n, i, :, side_at] = x * sign if FIELD_SIGNS[c] < 0 else x
            stress[n, i, :, :cols] = halo[n, i_main]
    for d in range(1, S_ROWS + 1):
        for x, i in zip(
            sides(len(VEL + NEAR + FAR) + d - 1), (S_ROWS - d, S_ROWS + rows - 1 + d)
        ):
            for n, value in enumerate(materials(x, dt, (density_t, lame_t, shear_t))):
                mats[n, i, :, side_at] = value
                mats[n, i, :, :cols] = mats_in[n, i, :, :cols]
    for n in range(3):
        for r in range(rows):
            mats[n, S_ROWS + r] = mats_in[n, S_ROWS + r]
    for k in range(6):
        for r in range(rows):
            vel[k, V_ROWS + r] = vel_in[k, r]

    vectors = level_vectors(levels, width, dr, theta_step)
    c1, c2 = vectors[1][:, :LANES], vectors[2][:, :LANES]

    def add_side(k, r, value):
        scale = mats[0, S_ROWS + r, :, side_at]
        vel[k, V_ROWS + r, :, side_at] = vel[k, V_ROWS + r, :, side_at] + scale * value

    for f in range(2):
        for c in range(3):
            k, n = f * 3 + c, f * 6 + CROSS[c] - 3
            n1, n2 = (stress[n, S_ROWS - d, :, side_at] for d in (1, 2))
            s1, s2 = (stress[n, S_ROWS + rows - 1 + d, :, side_at] for d in (1, 2))
            o1, o2 = (stress_in[n, S_ROWS + d, :, side_at] for d in (0, 1))
            u1, u2 = (stress_in[n, S_ROWS + rows - d, :, side_at] for d in (1, 2))
            add_side(k, 0, c2 * n2 - c1 * n1)
            add_side(k, 1, c2 * n1)
            add_side(k, rows - 1, c1 * s1 - c2 * s2)
            add_side(k, rows - 2, -(c2 * s1))
            add_side(k, -1, c1 * o1 - c2 * o2)
            add_side(k, -2, -(c2 * o1))
            add_side(k, rows, c2 * u2 - c1 * u1)
            add_side(k, rows + 1, c2 * u1)

    def first_stress(before, i, carry):
        row_ap, row_cv = widened(ap[i], width), widened(cv[i], width)
        lam, mu2 = mats[1, i], mats[2, i]
        for f in range(2):
            new = stress_steps(
                vel, f, i + V_ROWS - S_ROWS, vectors, row_ap, row_cv, lam, mu2, width
            )
            for n in range(6):
                stress[f * 6 + n, i] = before[f * 6 + n, i] + new[n]
        return carry

    inner = S_ROWS + rows
    lax.fori_loop(0, S_ROWS, functools.partial(first_stress, stress), 0, unroll=4)
    lax.fori_loop(S_ROWS, inner, functools.partial(first_stress, stress_in), 0, unroll=4)
    lax.fori_loop(inner, inner + S_ROWS, functools.partial(first_stress, stress), 0, unroll=4)

    def second_velocity(own, r, carry):
        i = r + S_ROWS - 2
        j = r + V_ROWS - 2
        row_ap, row_cv = widened(ap[i], width), widened(cv[i], width)
        scale = mats[0, i]
        fresh, products = [], []
        if own:
            for c in range(3):
                products.append(vel[c, j, :, :cols] * vel[3 + c, j, :, :cols])
        for f in range(2):
            for c, force in enumerate(forces(stress, f, i, vectors, row_ap, row_cv)):
                new = vel[f * 3 + c, j] + scale * force
                if f == 1 or c == 2:
                    new = new + second[f * (1 + c), r]
                vel[f * 3 + c, j] = new
                fresh.append(new[:, :cols])
        if own:
            for c in range(3):
                products.append(fresh[c] * fresh[3 + c])
            density[pl.ds(r - 2, levels, stride=rows), :] = sum(products[1:], products[0])
            for f in range(2):
                for c in range(3):
                    at = c * levels * rows + r - 2
                    (fwd, adj)[f][pl.ds(at, levels, stride=rows), :] = fresh[f * 3 + c]
        return carry

    lax.fori_loop(0, 2, functools.partial(second_velocity, False), 0, unroll=2)
    lax.fori_loop(2, rows + 2, functools.partial(second_velocity, True), 0, unroll=4)
    lax.fori_loop(rows + 2, rows + 4, functools.partial(second_velocity, False), 0, unroll=2)

    def second_stress(r, carry):
        i = r + S_ROWS
        row_ap, row_cv = widened(ap[i], cols), widened(cv[i], cols)
        lam, mu2 = mats[1, i, :, :cols], mats[2, i, :, :cols]
        for f in range(2):
            new = stress_steps(vel, f, r + V_ROWS, vectors, row_ap, row_cv, lam, mu2, cols)
            for n in range(6):
                at = (3 + n) * levels * rows + r
                (fwd, adj)[f][pl.ds(at, levels, stride=rows), :] = (
                    stress[f * 6 + n, i, :, :cols] + new[n]
                )
        return carry

    lax.fori_loop(0, rows, second_stress, 0, unroll=4)


def swap_tiles(x, first):
    count = lax.axis_size("lon")
    to = {i: (i + (1 if (i % 2 == 0) == first else -1)) % count for i in range(count)}
    return lax.ppermute(x, "lon", list(to.items()))


def swap_bands(x, first):
    bands, count = lax.axis_size("colat"), lax.axis_size("lon")
    pairs = []
    for lon in range(count):
        for band in range(bands):
            to_band, to_lon = band + (1 if (band % 2 == 0) == first else -1), lon
            if to_band < 0 or to_band >= bands:
                to_band, to_lon = band, (lon + count // 2) % count
            pairs.append((lon * bands + band, to_lon * bands + to_band))
    return lax.ppermute(x, ("lon", "colat"), pairs)


def call(kernel, out_shapes, specs, cost=0, limit=16 * 2**20, **more):
    return pl.pallas_call(
        kernel,
        out_shape=out_shapes,
        in_specs=specs,
        out_specs=jax.tree.map(lambda _: vmem(), out_shapes),
        cost_estimate=pl.CostEstimate(flops=cost, bytes_accessed=cost, transcendentals=0),
        compiler_params=pltpu.CompilerParams(vmem_limit_bytes=limit),
        **more,
    )


def on_device(
    forward_state, adjoint_state, layer_ids, density_table, lame_table, shear_table,
    source_cells, source_wavelet, receiver_cells, receiver_residual,
):
    dims = levels, rows, cols = layer_ids.shape
    lat_cells = rows * lax.axis_size("colat")
    lon_cells = cols * lax.axis_size("lon")
    dt = COURANT * SIN_FLOOR * R_INNER * (2.0 * math.pi / lon_cells) / 1.6
    consts = ((1.0 - R_INNER) / levels, math.pi / lat_cells, dt)
    width = cols + LANES
    tiles = cols // LANES

    def shape(*dims):
        return jax.ShapeDtypeStruct(dims, F32)

    parts = forward_state, adjoint_state, layer_ids.astype(F32)
    state = jnp.concatenate([x.reshape(-1, rows, cols) for x in parts]).reshape(-1, cols)

    edges = shape(pieces(19 * rows, EDGE), levels, LANES)
    near = shape(len(NEAR), levels, cols)
    far = shape(len(FAR) + S_ROWS, levels, cols)
    edge_a, edge_b, near_a, near_b, far_a, far_b = call(
        functools.partial(pack_kernel, dims),
        [edges, edges, near, near, far, far],
        [vmem()],
        cost=10**6,
    )(state)
    near_b, near_a = swap_bands(near_b, False), swap_bands(near_a, True)
    edge_b, edge_a = swap_tiles(edge_b, False), swap_tiles(edge_a, True)
    far_b = swap_bands(far_b, False)
    far_a = swap_bands(far_a, True)

    deep = shape(rows + 2 * S_ROWS, levels, LANES)
    count = max(LANES, receiver_cells.shape[0])

    def lines(x):
        x = x.astype(F32).reshape(-1, x.shape[-1])
        return jnp.pad(x, ((0, 0), (0, count - x.shape[1])))

    given = jnp.concatenate(
        [lines(x) for x in (receiver_cells, receiver_residual, source_cells, source_wavelet)]
    )
    extents = lat_cells, lon_cells
    first, ap, cv = call(
        functools.partial(first_inject_kernel, dims, extents),
        [shape(4, rows, levels, width), deep, deep],
        [vmem()],
        cost=10**8,
    )(given)

    extra = len(VEL + NEAR + FAR) + S_ROWS
    payload = shape(len(VEL) * tiles + pieces(extra, 2 * EDGE), levels, LANES)
    stress_shape = shape(12, rows + 2 * S_ROWS, levels, width)
    mats_shape = shape(3, rows + 2 * S_ROWS, levels, width)
    stress, vel, pay_a, pay_b = call(
        functools.partial(velocity_kernel, dims, consts),
        [stress_shape, shape(6, rows, levels, width), payload, payload],
        [vmem()] * 8 + [smem()],
        cost=10**7,
        scratch_shapes=[
            pltpu.VMEM((rows, levels, width), F32),
            pltpu.VMEM((rows, levels, LANES), F32),
        ],
    )(state, edge_a, edge_b, near_a, near_b, ap, cv, first, density_table)
    got_b, got_a = swap_bands(pay_b, False), swap_bands(pay_a, True)

    second = call(
        functools.partial(second_inject_kernel, dims, extents),
        shape(4, rows + 4, levels, width),
        [vmem()],
        cost=10**8,
    )(given)
    halo, mats = call(
        functools.partial(fill_kernel, dims, dt),
        [shape(12, 2 * S_ROWS, levels, cols), mats_shape],
        [vmem()] * 6 + [smem()] * 3,
        cost=10**8,
    )(stress, state, edge_a, edge_b, far_a, far_b, density_table, lame_table, shear_table)

    fwd, adj, density = call(
        functools.partial(final_kernel, dims, consts),
        [shape(9 * levels * rows, cols)] * 2 + [shape(levels * rows, cols)],
        [vmem()] * 9 + [smem()] * 3,
        cost=10**8,
        scratch_shapes=[
            pltpu.VMEM((6, rows + 2 * V_ROWS, levels, width), F32),
            pltpu.VMEM(stress_shape.shape, F32),
            pltpu.VMEM(mats_shape.shape, F32),
        ],
    )(
        vel, stress, halo, got_a, got_b, mats, second, ap, cv,
        density_table, lame_table, shear_table,
    )
    return (
        fwd.reshape(forward_state.shape),
        adj.reshape(adjoint_state.shape),
        density.reshape(layer_ids.shape),
    )


def solution(mesh):
    return jax.shard_map(
        on_device,
        mesh=mesh,
        in_specs=(
            P(None, None, "colat", "lon"),
            P(None, None, "colat", "lon"),
            P(None, "colat", "lon"),
        )
        + (P(),) * 7,
        out_specs=(
            P(None, None, "colat", "lon"),
            P(None, None, "colat", "lon"),
            P(None, "colat", "lon"),
        ),
        check_vma=False,
    )
```

profile of v0, /device:TPU:0, one launch (start us, length us, event | category | flops | bytes accessed | tf_op | source)
XLA Modules:
  0.0 40.7 jit_solution(17873357959160000785)
XLA Ops:
  0.6 0.8 %convert_element_type.13 = f32[8,16,128]{2,1,0:T(8,128)S(1)} convert(s32[8,16,128]{2,1,0:T(8,128)} %param.12) | non-fusion elementwise | flops 16384 | bytes 131072 | tf_op jit(solution)/shard_map/convert_element_type | solution.py:639
  1.5 1.3 %pad_maximum_fusion = f32[152,16,128]{2,1,0:T(8,128)S(1)} fusion(f32[8,16,128]{2,1,0:T(8,128)S(1)} %convert_element_type.13, f32[72,16,128]{2,1,0:T(8,128)} %bitcast.12, f32[72,16,128]{2,1,0:T(8,128)} %bitcast.13), kind=kLoop, calls=%fused_computation | loop fusion | flops 622592 | bytes 2490368 | tf_op jit(solution)/shard_map/concatenate | solution.py:640
  2.8 0.0 copy-start.3
  2.8 0.0 copy-start.4
  2.8 0.0 copy-start.6
  2.8 0.0 copy-start.5
  2.9 0.0 copy-start
  2.9 0.7 %shard_map.121 = (f32[19,8,128]{2,1,0:T(8,128)S(1)}, f32[19,8,128]{2,1,0:T(8,128)S(1)}, f32[12,8,128]{2,1,0:T(8,128)S(1)}, f32[12,8,128]{2,1,0:T(8,128)S(1)}, f3...) custom-call(f32[2432,128]{1,0:T(8,128)S(1)} %bitcast.9), custom_call_target="tpu_custom_call" | custom-call | flops 1000000 | bytes 1000000 | tf_op jit(solution)/shard_map/pallas_call | solution.py:645
  3.6 0.6 %collective-permute-start = (f32[19,8,128]{2,1,0:T(8,128)S(1)}, f32[19,8,128]{2,1,0:T(8,128)S(1)}, u32[]{:S(2)}, u32[]{:S(2)}) collective-permute-start(f32[19,8,128]{2,1,0:T(8,128)S(1)} %get-tuple-element.21), channel_id=1, source_target_pairs={{0,4},{4,0},{8,12},{12,8},{16,20},{20,16},{24,28},{28,24},{1,5},{5... | collective-permute-start | bytes 233480 | tf_op jit(solution)/shard_map/ppermute | solution.py:597
  4.1 4.7 %collective-permute-start.1 = (f32[19,8,128]{2,1,0:T(8,128)S(1)}, f32[19,8,128]{2,1,0:T(8,128)S(1)}, u32[]{:S(2)}, u32[]{:S(2)}) collective-permute-start(f32[19,8,128]{2,1,0:T(8,128)S(1)} %get-tuple-element.22), channel_id=1, source_target_pairs={{0,28},{4,8},{8,4},{12,16},{16,12},{20,24},{24,20},{28,0},{1,29},{... | collective-permute-start | bytes 233480 | tf_op jit(solution)/shard_map/ppermute | solution.py:597
  8.8 1.5 %collective-permute-start.2 = (f32[12,8,128]{2,1,0:T(8,128)S(1)}, f32[12,8,128]{2,1,0:T(8,128)S(1)}, u32[]{:S(2)}, u32[]{:S(2)}) collective-permute-start(f32[12,8,128]{2,1,0:T(8,128)S(1)} %get-tuple-element.23), channel_id=1, source_target_pairs={{0,1},{1,0},{2,3},{3,2},{4,5},{5,4},{6,7},{7,6},{8,9},{9,8},{10,11... | collective-permute-start | bytes 147464 | tf_op jit(solution)/shard_map/ppermute | solution.py:609
  10.3 0.0 collective-permute-start.3
  10.3 0.0 copy-done.3
  10.3 0.0 copy-done.4
  10.4 0.0 copy-done.6
  10.4 0.0 copy-done.5
  10.4 0.9 %shard_map.122 = (f32[4,16,8,256]{3,2,1,0:T(8,128)S(1)}, f32[24,8,128]{2,1,0:T(8,128)S(1)}, f32[24,8,128]{2,1,0:T(8,128)S(1)}) custom-call(f32[10,512]{1,0:T(8,128)S(1)} %select_maximum_fusion.given), custom_call_target="tpu_custom_call" | custom-call | flops 100000000 | bytes 100000000 | tf_op jit(solution)/shard_map/pallas_call | solution.py:667
  11.3 1.6 %collective-permute-done.2.near_a = f32[12,8,128]{2,1,0:T(8,128)S(1)} collective-permute-done((f32[12,8,128]{2,1,0:T(8,128)S(1)}, f32[12,8,128]{2,1,0:T(8,128)S(1)}, u32[]{:S(2)}, u32[]{:S(2)}) %collective-permute-start.2) | collective-permute-done | bytes 49184 | tf_op jit(solution)/shard_map/ppermute | solution.py:609
  12.9 2.4 %collective-permute-done.3.near_b = f32[12,8,128]{2,1,0:T(8,128)S(1)} collective-permute-done((f32[12,8,128]{2,1,0:T(8,128)S(1)}, f32[12,8,128]{2,1,0:T(8,128)S(1)}, u32[]{:S(2)}, u32[]{:S(2)}) %collective-permute-start.3) | collective-permute-done | bytes 49184 | tf_op jit(solution)/shard_map/ppermute | solution.py:609
  15.3 0.0 collective-permute-done.edge_a.id_edge_a
  15.3 0.0 collective-permute-done.1.edge_b.id_edge_b
  15.3 0.0 copy-done
  15.3 0.0 copy-start.1
  15.3 0.0 copy-start.2
  15.3 3.4 %shard_map.123 = (f32[12,24,8,256]{3,2,1,0:T(8,128)S(1)}, f32[6,16,8,256]{3,2,1,0:T(8,128)S(1)}, f32[46,8,128]{2,1,0:T(8,128)S(1)}, f32[46,8,128]{2,1,0:T(8,128)S(1)}) custom-call(f32[2432,128]{1,0:T(8,128)S(1)} %bitcast.10, f32[19,8,128]{2,1,0:T(8,128)S(1)} %collective-permute-done.edge_a.id_edge_a, ...), custom_call_target="tpu_custom_call" | custom-call | flops 10000000 | bytes 10000000 | tf_op jit(solution)/shard_map/pallas_call | solution.py:678
  18.8 0.6 %collective-permute-start.6 = (f32[46,8,128]{2,1,0:T(8,128)S(1)}, f32[46,8,128]{2,1,0:T(8,128)S(1)}, u32[]{:S(2)}, u32[]{:S(2)}) collective-permute-start(f32[46,8,128]{2,1,0:T(8,128)S(1)} %get-tuple-element.33), channel_id=1, source_target_pairs={{0,1},{1,0},{2,3},{3,2},{4,5},{5,4},{6,7},{7,6},{8,9},{9,8},{10,11... | collective-permute-start | bytes 565256 | tf_op jit(solution)/shard_map/ppermute | solution.py:609
  19.4 0.3 collective-permute-start.7
  19.7 2.7 %collective-permute-start.4 = (f32[28,8,128]{2,1,0:T(8,128)S(1)}, f32[28,8,128]{2,1,0:T(8,128)S(1)}, u32[]{:S(2)}, u32[]{:S(2)}) collective-permute-start(f32[28,8,128]{2,1,0:T(8,128)S(1)} %get-tuple-element.30), channel_id=1, source_target_pairs={{0,1},{1,0},{2,3},{3,2},{4,5},{5,4},{6,7},{7,6},{8,9},{9,8},{10,11... | collective-permute-start | bytes 344072 | tf_op jit(solution)/shard_map/ppermute | solution.py:609
  22.4 0.9 %collective-permute-start.5 = (f32[28,8,128]{2,1,0:T(8,128)S(1)}, f32[28,8,128]{2,1,0:T(8,128)S(1)}, u32[]{:S(2)}, u32[]{:S(2)}) collective-permute-start(f32[28,8,128]{2,1,0:T(8,128)S(1)} %get-tuple-element.31), channel_id=1, source_target_pairs={{0,16},{1,2},{2,1},{3,19},{4,20},{5,6},{6,5},{7,23},{8,24},{9,10},... | collective-permute-start | bytes 344072 | tf_op jit(solution)/shard_map/ppermute | solution.py:609
  23.2 2.1 %shard_map.125.second = f32[4,20,8,256]{3,2,1,0:T(8,128)S(1)} custom-call(f32[10,512]{1,0:T(8,128)S(1)} %select_maximum_fusion.given), custom_call_target="tpu_custom_call" | custom-call | flops 100000000 | bytes 100000000 | tf_op jit(solution)/shard_map/pallas_call | solution.py:690
  25.4 5.6 %collective-permute-done.4.far_a = f32[28,8,128]{2,1,0:T(8,128)S(1)} collective-permute-done((f32[28,8,128]{2,1,0:T(8,128)S(1)}, f32[28,8,128]{2,1,0:T(8,128)S(1)}, u32[]{:S(2)}, u32[]{:S(2)}) %collective-permute-start.4) | collective-permute-done | bytes 114720 | tf_op jit(solution)/shard_map/ppermute | solution.py:609
  30.9 2.4 %collective-permute-done.5.far_b = f32[28,8,128]{2,1,0:T(8,128)S(1)} collective-permute-done((f32[28,8,128]{2,1,0:T(8,128)S(1)}, f32[28,8,128]{2,1,0:T(8,128)S(1)}, u32[]{:S(2)}, u32[]{:S(2)}) %collective-permute-start.5) | collective-permute-done | bytes 114720 | tf_op jit(solution)/shard_map/ppermute | solution.py:609
  33.4 0.0 copy-done.1
  33.4 0.0 copy-done.2
  33.4 1.0 %shard_map.124 = (f32[12,8,8,128]{3,2,1,0:T(8,128)S(1)}, f32[3,24,8,256]{3,2,1,0:T(8,128)S(1)}) custom-call(f32[12,24,8,256]{3,2,1,0:T(8,128)S(1)} %get-tuple-element.29.stress.stress_in, f32[2432,128]{1,0:T(8,128)S(1)} %bitcast.11, f32[19,8,128]{2,1,0:T(8,128)S(1)} %collective-permute-done.edge_a.id_edge_a, ...), custom_call_target="tpu_custom_call" | custom-call | flops 100000000 | bytes 100000000 | tf_op jit(solution)/shard_map/pallas_call | solution.py:696
  34.4 0.0 collective-permute-done.6.got_a
  34.4 0.0 collective-permute-done.7.got_b
  34.4 6.3 %shard_map.126 = (f32[1152,128]{1,0:T(8,128)}, f32[1152,128]{1,0:T(8,128)}, f32[128,128]{1,0:T(8,128)}) custom-call(f32[6,16,8,256]{3,2,1,0:T(8,128)S(1)} %get-tuple-element.28.vel_in, f32[12,24,8,256]{3,2,1,0:T(8,128)S(1)} %get-tuple-element.29.stress.stress_in, f32[12,8,8,128]{3,2,1,0:T(8,128)S(1)} %get-tuple-element.32.halo, ...), custom_call_target="tpu_custom_call" | custom-call | flops 100000000 | bytes 100000000 | tf_op jit(solution)/shard_map/pallas_call | solution.py:703
  (5 shorter events, 0.0 us)
Async XLA Ops:
  2.8 7.5 %copy-start.3 = (f32[2,3,512]{2,0,1:T(2,128)S(1)}, f32[2,3,512]{2,0,1:T(2,128)}, u32[]{:S(2)}) copy-start(f32[2,3,512]{2,0,1:T(2,128)} %param.19) | copy-start | bytes 36868
  2.8 7.5 %copy-start.4 = (s32[512]{0:T(512)S(1)}, s32[512]{0:T(512)}, u32[]{:S(2)}) copy-start(s32[512]{0:T(512)} %param.18) | copy-start | bytes 6148
  2.8 7.5 %copy-start.6 = (s32[8]{0:T(128)S(1)}, s32[8]{0:T(128)}, u32[]{:S(2)}) copy-start(s32[8]{0:T(128)} %param.16) | copy-start | bytes 100
  2.8 7.6 %copy-start.5 = (f32[2,8]{1,0:T(2,128)S(1)}, f32[2,8]{1,0:T(2,128)}, u32[]{:S(2)}) copy-start(f32[2,8]{1,0:T(2,128)} %param.17) | copy-start | bytes 196
  2.9 12.5 %copy-start = (f32[16]{0:T(128)S(1)}, f32[16]{0:T(128)}, u32[]{:S(2)}) copy-start(f32[16]{0:T(128)} %density_t.1) | copy-start | bytes 196
  3.6 11.7 %collective-permute-start = (f32[19,8,128]{2,1,0:T(8,128)S(1)}, f32[19,8,128]{2,1,0:T(8,128)S(1)}, u32[]{:S(2)}, u32[]{:S(2)}) collective-permute-start(f32[19,8,128]{2,1,0:T(8,128)S(1)} %get-tuple-element.21), channel_id=1, source_target_pairs={{0,4},{4,0},{8,12},{12,8},{16,20},{20,16},{24,28},{28,24},{1,5},{5... | collective-permute-start | bytes 233480 | tf_op jit(solution)/shard_map/ppermute | solution.py:597
  4.1 11.2 %collective-permute-start.1 = (f32[19,8,128]{2,1,0:T(8,128)S(1)}, f32[19,8,128]{2,1,0:T(8,128)S(1)}, u32[]{:S(2)}, u32[]{:S(2)}) collective-permute-start(f32[19,8,128]{2,1,0:T(8,128)S(1)} %get-tuple-element.22), channel_id=1, source_target_pairs={{0,28},{4,8},{8,4},{12,16},{16,12},{20,24},{24,20},{28,0},{1,29},{... | collective-permute-start | bytes 233480 | tf_op jit(solution)/shard_map/ppermute | solution.py:597
  8.8 4.1 %collective-permute-start.2 = (f32[12,8,128]{2,1,0:T(8,128)S(1)}, f32[12,8,128]{2,1,0:T(8,128)S(1)}, u32[]{:S(2)}, u32[]{:S(2)}) collective-permute-start(f32[12,8,128]{2,1,0:T(8,128)S(1)} %get-tuple-element.23), channel_id=1, source_target_pairs={{0,1},{1,0},{2,3},{3,2},{4,5},{5,4},{6,7},{7,6},{8,9},{9,8},{10,11... | collective-permute-start | bytes 147464 | tf_op jit(solution)/shard_map/ppermute | solution.py:609
  10.3 5.0 %collective-permute-start.3 = (f32[12,8,128]{2,1,0:T(8,128)S(1)}, f32[12,8,128]{2,1,0:T(8,128)S(1)}, u32[]{:S(2)}, u32[]{:S(2)}) collective-permute-start(f32[12,8,128]{2,1,0:T(8,128)S(1)} %get-tuple-element.24), channel_id=1, source_target_pairs={{0,16},{1,2},{2,1},{3,19},{4,20},{5,6},{6,5},{7,23},{8,24},{9,10},... | collective-permute-start | bytes 147464 | tf_op jit(solution)/shard_map/ppermute | solution.py:609
  15.3 18.0 %copy-start.1 = (f32[16]{0:T(128)S(1)}, f32[16]{0:T(128)}, u32[]{:S(2)}) copy-start(f32[16]{0:T(128)} %lame_t.1) | copy-start | bytes 196
  15.3 18.0 %copy-start.2 = (f32[16]{0:T(128)S(1)}, f32[16]{0:T(128)}, u32[]{:S(2)}) copy-start(f32[16]{0:T(128)} %shear_t.1) | copy-start | bytes 196
  18.8 15.6 %collective-permute-start.6 = (f32[46,8,128]{2,1,0:T(8,128)S(1)}, f32[46,8,128]{2,1,0:T(8,128)S(1)}, u32[]{:S(2)}, u32[]{:S(2)}) collective-permute-start(f32[46,8,128]{2,1,0:T(8,128)S(1)} %get-tuple-element.33), channel_id=1, source_target_pairs={{0,1},{1,0},{2,3},{3,2},{4,5},{5,4},{6,7},{7,6},{8,9},{9,8},{10,11... | collective-permute-start | bytes 565256 | tf_op jit(solution)/shard_map/ppermute | solution.py:609
  19.4 15.0 %collective-permute-start.7 = (f32[46,8,128]{2,1,0:T(8,128)S(1)}, f32[46,8,128]{2,1,0:T(8,128)S(1)}, u32[]{:S(2)}, u32[]{:S(2)}) collective-permute-start(f32[46,8,128]{2,1,0:T(8,128)S(1)} %get-tuple-element.34), channel_id=1, source_target_pairs={{0,16},{1,2},{2,1},{3,19},{4,20},{5,6},{6,5},{7,23},{8,24},{9,10},... | collective-permute-start | bytes 565256 | tf_op jit(solution)/shard_map/ppermute | solution.py:609
  19.7 11.2 %collective-permute-start.4 = (f32[28,8,128]{2,1,0:T(8,128)S(1)}, f32[28,8,128]{2,1,0:T(8,128)S(1)}, u32[]{:S(2)}, u32[]{:S(2)}) collective-permute-start(f32[28,8,128]{2,1,0:T(8,128)S(1)} %get-tuple-element.30), channel_id=1, source_target_pairs={{0,1},{1,0},{2,3},{3,2},{4,5},{5,4},{6,7},{7,6},{8,9},{9,8},{10,11... | collective-permute-start | bytes 344072 | tf_op jit(solution)/shard_map/ppermute | solution.py:609
  22.4 11.0 %collective-permute-start.5 = (f32[28,8,128]{2,1,0:T(8,128)S(1)}, f32[28,8,128]{2,1,0:T(8,128)S(1)}, u32[]{:S(2)}, u32[]{:S(2)}) collective-permute-start(f32[28,8,128]{2,1,0:T(8,128)S(1)} %get-tuple-element.31), channel_id=1, source_target_pairs={{0,16},{1,2},{2,1},{3,19},{4,20},{5,6},{6,5},{7,23},{8,24},{9,10},... | collective-permute-start | bytes 344072 | tf_op jit(solution)/shard_map/ppermute | solution.py:609
where the time goes:
time: 40.9 us; the launch traced here: 40.7 us
  Pallas kernels  14.5 us (35%)
  waiting for transfers between devices  12 us (29%)
  starting transfers between devices  11.2 us (27%)
  other arithmetic  2.19 us (5%)
  between operations  0.8 us (2%)
    ppermute x6, waiting for transfers between devices, swap_bands(): return lax.ppermute(x, ('lon', 'colat'), pairs)  12 us
    pallas_call x1, Pallas kernels, on_device(): call(functools.partial(final_kernel, dims, consts), [shape(9 * levels * r...  6.27 us
    ppermute x6, starting transfers between devices, swap_bands(): return lax.ppermute(x, ('lon', 'colat'), pairs)  5.92 us
    ppermute x2, starting transfers between devices, swap_tiles(): return lax.ppermute(x, 'lon', list(to.items()))  5.26 us
    pallas_call x1, Pallas kernels, on_device(): call(functools.partial(velocity_kernel, dims, consts), [stress_shape, sha...  3.43 us
    pallas_call x1, Pallas kernels, on_device(): call(functools.partial(second_inject_kernel, dims, extents), shape(4, row...  2.13 us
    concatenate x1, other arithmetic, on_device(): jnp.concatenate([x.reshape(-1, rows, cols) for x in parts])  1.32 us
    pallas_call x1, Pallas kernels, on_device(): call(functools.partial(fill_kernel, dims, dt), [shape(12, 2 * S_ROWS, lev...  1.04 us
  transfers between devices with their start and end apart: 8, of which 4 were waited for; matrix products, arithmetic and copies ran while one was open for 0% of the time, Pallas kernels for 10%

commit v1 on v0

--- a/solution.py
+++ b/solution.py
@@ -18,6 +18,7 @@
 LANES = 128
 V_ROWS = 6
 S_ROWS = 4
+INNER = 4
 F32 = jnp.float32
 
 
@@ -47,27 +48,17 @@
     return x if shift == 0 else pltpu.roll(x, shift, axis)
 
 
-class Packer:
-    def __init__(self, ref, width, base=0):
-        self.ref, self.width, self.base = ref, width, base
-        self.per = LANES // width
-        self.count, self.value = 0, None
-
-    def add(self, x, start):
-        slot = self.count % self.per
-        moved = rolled(x, slot * self.width - start)
-        if slot == 0:
-            self.value = moved
-        else:
-            self.value = jnp.where(lane_iota(x.shape) >= slot * self.width, moved, self.value)
-        self.count += 1
-        if self.count % self.per == 0:
-            self.flush()
-
-    def flush(self):
-        if self.value is not None:
-            self.ref[self.base + (self.count - 1) // self.per] = self.value
-            self.value = None
+def side_plan():
+    wide = [("v", f, c, 1) for f in range(2) for c in range(3)]
+    wide += [("s",) + entry for entry in NEAR] + [("i", 0, 0, 1)]
+    slim = [("v", f, c, d) for f, c, d in VEL if 1 < d < V_ROWS]
+    slim += [("s",) + entry for entry in FAR if entry[2] < S_ROWS] + [("i", 0, 0, 2), ("i", 0, 0, 3)]
+    plan, lane = {}, 0
+    for width, entries in ((2 * EDGE, wide), (EDGE, slim)):
+        for entry in entries:
+            plan[entry] = (lane // LANES, lane % LANES, width)
+            lane += width
+    return plan, -(-lane // LANES)
 
 
 def pieces(count, width):
@@ -75,10 +66,16 @@
     return -(-count // per)
 
 
-def halo_vector(east, west, slot):
-    after = rolled(east, -slot * EDGE)
-    before = rolled(west, LANES - EDGE - slot * EDGE)
-    return jnp.where(lane_iota(after.shape) < LANES // 2, after, before)
+def paired_edges(edge_a, edge_b, v):
+    a, b = edge_a[v], edge_b[v]
+    even = even_tile()
+    after, before = jnp.where(even, a, b), jnp.where(even, b, a)
+    odd_lane = lax.rem(lane_iota(a.shape) // EDGE, 2) == 1
+    return jnp.where(odd_lane, before, after), jnp.where(odd_lane, after, before)
+
+
+def side_vector(paired, slot):
+    return rolled(paired[slot % 2], -slot * EDGE)
 
 
 def even_band():
@@ -100,7 +97,7 @@
     return ref[pl.ds(first, levels, stride=rows), :]
 
 
-def pack_kernel(dims, state, edge_a, edge_b, near_a, near_b, far_a, far_b):
+def pack_kernel(dims, state, ids, edge_a, edge_b, near_a, near_b, far_a, far_b):
     levels, rows, cols = dims
     even = even_band()
 
@@ -108,7 +105,7 @@
         return strided(state, (f * 9 + c) * levels * rows + r, levels, rows)
 
     def id_row(r):
-        return strided(state, 18 * levels * rows + r, levels, rows)
+        return strided(ids, r, levels, rows).astype(F32)
 
     def put(ref_a, ref_b, k, get, d):
         top, bottom = get(d - 1), get(rows - d)
@@ -121,25 +118,27 @@
     for d in range(1, S_ROWS + 1):
         put(far_a, far_b, FAR_IDS + d - 1, id_row, d)
 
-    east, west = Packer(edge_a, EDGE), Packer(edge_b, EDGE)
-
-    def both(x):
-        east.add(x[:, cols - LANES :], LANES - EDGE)
-        west.add(x[:, :LANES], 0)
-
-    for f in range(2):
-        for c in range(9):
-            for r in range(rows):
-                both(row(f, c, r))
-    for r in range(rows):
-        both(id_row(r))
-    east.flush()
-    west.flush()
-
-    @pl.when(jnp.logical_not(even_tile()))
-    def _():
-        for v in range(edge_a.shape[0]):
-            edge_a[v], edge_b[v] = edge_b[v], edge_a[v]
+    per = LANES // EDGE
+    edges = [functools.partial(row, f, c, r) for f in range(2) for c in range(9) for r in range(rows)]
+    edges += [functools.partial(id_row, r) for r in range(rows)]
+    lane = lane_iota((levels, LANES))
+    swapped = jnp.logical_not(even_tile())
+    for v in range(edge_a.shape[0]):
+        east = west = None
+        for slot, get in reversed(list(enumerate(edges[v * per : (v + 1) * per]))):
+            x = get()
+            last = rolled(x[:, cols - LANES :], slot * EDGE)
+            first = last if cols == LANES else rolled(x[:, :LANES], slot * EDGE)
+            if east is None:
+                east, west = last, first
+            else:
+                west = jnp.where(lane < (slot + 1) * EDGE, first, west)
+                if slot:
+                    east = jnp.where(lane < slot * EDGE, last, east)
+                else:
+                    east = jnp.where(lane < LANES - EDGE, east, last)
+        edge_a[v] = jnp.where(swapped, west, east)
+        edge_b[v] = jnp.where(swapped, east, west)
 
 
 def divided(x, by):
@@ -341,7 +340,7 @@
 
 
 def velocity_kernel(
-    dims, consts, state, edge_a, edge_b, near_a, near_b, ap, cv, first, density,
+    dims, consts, state, ids, edge_a, edge_b, near_a, near_b, ap, cv, first, density,
     stress, vel, pay_a, pay_b, rho, id_side,
 ):
     levels, rows, cols = dims
@@ -350,11 +349,12 @@
     signs = pole_signs()
     even = even_band()
     per = LANES // EDGE
-    east_first = even_tile()
+    paired = {}
 
     def side_of(j):
-        a, b = edge_a[j // per], edge_b[j // per]
-        return halo_vector(jnp.where(east_first, a, b), jnp.where(east_first, b, a), j % per)
+        if j // per not in paired:
+            paired[j // per] = paired_edges(edge_a, edge_b, j // per)
+        return side_vector(paired[j // per], j % per)
 
     for f in range(2):
         for c in range(9):
@@ -368,7 +368,7 @@
                 ref[k, i, :, :cols] = main
                 ref[k, i, :, cols:] = side
     for r in range(rows):
-        main = strided(state, 18 * levels * rows + r, levels, rows)
+        main = strided(ids, r, levels, rows).astype(F32)
         side = side_of(18 * rows + r)
         id_side[r] = side
         rho[r, :, :cols] = dt / look_up(main, (density,))[0]
@@ -396,36 +396,44 @@
                 vel[f * 3 + c, r] = new
         return carry
 
-    lax.fori_loop(0, rows, step, 0, unroll=2)
+    lax.fori_loop(0, rows, step, 0, unroll=8)
 
     tiles = cols // LANES
+    plan, vectors_out = side_plan()
     for ref, bottom_side in ((pay_a, even), (pay_b, jnp.logical_not(even))):
-        packer = Packer(ref, 2 * EDGE, len(VEL) * tiles)
 
         def facing(d):
             return jnp.where(bottom_side, rows - d, d - 1)
 
         for k, (f, c, d) in enumerate(VEL):
-            x = vel[f * 3 + c, facing(d)]
             for t in range(tiles):
-                ref[k * tiles + t] = x[:, t * LANES : (t + 1) * LANES]
-            packer.add(x[:, cols:], LANES - EDGE)
-        for f, c, d in NEAR + FAR:
-            packer.add(stress[f * 6 + c - 3, facing(d) + S_ROWS, :, cols:], LANES - EDGE)
-        for d in range(1, S_ROWS + 1):
-            packer.add(id_side[facing(d)], LANES - EDGE)
-        packer.flush()
+                at = slice(t * LANES, (t + 1) * LANES)
+                ref[k * tiles + t] = vel[f * 3 + c, facing(d), :, at]
+        packed, lanes = [None] * vectors_out, lane_iota((levels, LANES))
+        for (kind, f, c, d), (v, lane, wide) in plan.items():
+            if kind == "v":
+                x = vel[f * 3 + c, facing(d), :, cols:]
+            elif kind == "s":
+                x = stress[f * 6 + c - 3, facing(d) + S_ROWS, :, cols:]
+            else:
+                x = id_side[facing(d)]
+            x = rolled(x, lane + wide // 2)
+            packed[v] = x if packed[v] is None else jnp.where(lanes >= lane, x, packed[v])
+        for v, x in enumerate(packed):
+            ref[len(VEL) * tiles + v] = x
 
 
 def fill_kernel(
-    dims, dt, stress, state, id_edge_a, id_edge_b, far_a, far_b, density, lame, shear,
-    halo, mats,
+    dims, consts, stress, vel, ids, id_edge_a, id_edge_b, far_a, far_b, second, ap, cv,
+    density, lame, shear, halo, mats, inner_stress, inner_vel, inner_density,
 ):
     levels, rows, cols = dims
+    dr, theta_step, dt = consts
+    width = cols + LANES
     signs = pole_signs()
     tables = density, lame, shear
     per = LANES // EDGE
-    east_first = even_tile()
+    paired = {}
 
     for k, (f, c, d) in enumerate(FAR):
         for main, i, sign in zip(
@@ -443,35 +451,70 @@
 
     main, side = slice(0, cols), slice(cols, cols + LANES)
     for r in range(rows):
-        material(r + S_ROWS, strided(state, 18 * levels * rows + r, levels, rows), main)
-        j = 18 * rows + r
-        a, b = id_edge_a[j // per], id_edge_b[j // per]
-        x = halo_vector(jnp.where(east_first, a, b), jnp.where(east_first, b, a), j % per)
-        material(r + S_ROWS, x, side)
+        material(r + S_ROWS, strided(ids, r, levels, rows).astype(F32), main)
+        v, slot = divmod(18 * rows + r, per)
+        if v not in paired:
+            paired[v] = paired_edges(id_edge_a, id_edge_b, v)
+        material(r + S_ROWS, side_vector(paired[v], slot), side)
     for d in range(1, S_ROWS + 1):
         north, south = north_south(far_a, far_b, FAR_IDS + d - 1)
         material(S_ROWS - d, north, main)
         material(S_ROWS + rows - 1 + d, south, main)
 
+    vectors = level_vectors(levels, width, dr, theta_step)
+
+    def inner_first(r, carry):
+        i = r + S_ROWS
+        row_ap, row_cv = widened(ap[i], width), widened(cv[i], width)
+        for f in range(2):
+            new = stress_steps(vel, f, r, vectors, row_ap, row_cv, mats[1, i], mats[2, i], width)
+            for n in range(6):
+                inner_stress[f * 6 + n, r - INNER] = stress[f * 6 + n, i] + new[n]
+        return carry
+
+    lax.fori_loop(INNER, rows - INNER, inner_first, 0, unroll=4)
+
+    def inner_second(r, carry):
+        i = r + S_ROWS
+        at = r - INNER - 2
+        row_ap, row_cv = widened(ap[i], width), widened(cv[i], width)
+        products = [vel[c, r, :, :cols] * vel[3 + c, r, :, :cols] for c in range(3)]
+        fresh = []
+        for f in range(2):
+            steps = forces(inner_stress, f, r - INNER, vectors, row_ap, row_cv)
+            for c, force in enumerate(steps):
+                new = vel[f * 3 + c, r] + mats[0, i] * force
+                if f == 1 or c == 2:
+                    new = new + second[f * (1 + c), r + 2]
+                inner_vel[f * 3 + c, at] = new
+                fresh.append(new[:, :cols])
+        products += [fresh[c] * fresh[3 + c] for c in range(3)]
+        inner_density[at] = sum(products[1:], products[0])
+        return carry
+
+    lax.fori_loop(INNER + 2, rows - INNER - 2, inner_second, 0, unroll=4)
+
 
 def final_kernel(
     dims, consts, vel_in, stress_in, halo, got_a, got_b, mats_in, second, ap, cv,
-    density_t, lame_t, shear_t, fwd, adj, density, vel, stress, mats,
+    inner_stress, inner_vel, inner_density, density_t, lame_t, shear_t,
+    fwd_out, adj_out, density_out, vel, stress, mats, fwd, adj, density, sems,
 ):
     levels, rows, cols = dims
     dr, theta_step, dt = consts
     width = cols + LANES
     signs = pole_signs()
     tiles = cols // LANES
-    per = LANES // (2 * EDGE)
-    even = even_band()
     side_at = slice(cols, width)
-
-    def sides(j):
-        v = len(VEL) * tiles + j // per
-        return (
-            rolled(x, -EDGE - (j % per) * 2 * EDGE) for x in north_south(got_a, got_b, v)
-        )
+    plan, _ = side_plan()
+    lanes_shape = (levels, LANES)
+
+    def sides(kind, f, c, d):
+        if (kind, f, c, d) not in plan:
+            return (jnp.zeros(lanes_shape, F32),) * 2
+        v, lane, wide = plan[kind, f, c, d]
+        got = north_south(got_a, got_b, len(VEL) * tiles + v)
+        return tuple(rolled(x, -lane - wide // 2) for x in got)
 
     for k, (f, c, d) in enumerate(VEL):
         flip = FIELD_SIGNS[c] < 0
@@ -480,12 +523,13 @@
             north, south = north_south(got_a, got_b, k * tiles + t)
             vel[f * 3 + c, V_ROWS - d, :, at] = north * signs[0] if flip else north
             vel[f * 3 + c, V_ROWS + rows - 1 + d, :, at] = south * signs[1] if flip else south
-        for x, i, sign in zip(sides(k), (V_ROWS - d, V_ROWS + rows - 1 + d), signs):
+        at = V_ROWS - d, V_ROWS + rows - 1 + d
+        for x, i, sign in zip(sides("v", f, c, d), at, signs):
             vel[f * 3 + c, i, :, side_at] = x * sign if flip else x
-    for k, (f, c, d) in enumerate(NEAR + FAR):
+    for f, c, d in NEAR + FAR:
         n = f * 6 + c - 3
         for x, i, i_main, sign in zip(
-            sides(len(VEL) + k),
+            sides("s", f, c, d),
             (S_ROWS - d, S_ROWS + rows - 1 + d),
             (S_ROWS - d, S_ROWS - 1 + d),
             signs,
@@ -493,9 +537,7 @@
             stress[n, i, :, side_at] = x * sign if FIELD_SIGNS[c] < 0 else x
             stress[n, i, :, :cols] = halo[n, i_main]
     for d in range(1, S_ROWS + 1):
-        for x, i in zip(
-            sides(len(VEL + NEAR + FAR) + d - 1), (S_ROWS - d, S_ROWS + rows - 1 + d)
-        ):
+        for x, i in zip(sides("i", 0, 0, d), (S_ROWS - d, S_ROWS + rows - 1 + d)):
             for n, value in enumerate(materials(x, dt, (density_t, lame_t, shear_t))):
                 mats[n, i, :, side_at] = value
                 mats[n, i, :, :cols] = mats_in[n, i, :, :cols]
@@ -505,6 +547,9 @@
     for k in range(6):
         for r in range(rows):
             vel[k, V_ROWS + r] = vel_in[k, r]
+    for n in range(12):
+        for r in range(INNER, rows - INNER):
+            stress[n, S_ROWS + r] = inner_stress[n, r - INNER]
 
     vectors = level_vectors(levels, width, dr, theta_step)
     c1, c2 = vectors[1][:, :LANES], vectors[2][:, :LANES]
@@ -542,7 +587,9 @@
 
     inner = S_ROWS + rows
     lax.fori_loop(0, S_ROWS, functools.partial(first_stress, stress), 0, unroll=4)
-    lax.fori_loop(S_ROWS, inner, functools.partial(first_stress, stress_in), 0, unroll=4)
+    outer = functools.partial(first_stress, stress_in)
+    lax.fori_loop(S_ROWS, S_ROWS + INNER, outer, 0, unroll=4)
+    lax.fori_loop(inner - INNER, inner, outer, 0, unroll=4)
     lax.fori_loop(inner, inner + S_ROWS, functools.partial(first_stress, stress), 0, unroll=4)
 
     def second_velocity(own, r, carry):
@@ -571,9 +618,29 @@
                     (fwd, adj)[f][pl.ds(at, levels, stride=rows), :] = fresh[f * 3 + c]
         return carry
 
+    reach = INNER + 2
+    own = functools.partial(second_velocity, True)
     lax.fori_loop(0, 2, functools.partial(second_velocity, False), 0, unroll=2)
-    lax.fori_loop(2, rows + 2, functools.partial(second_velocity, True), 0, unroll=4)
+    lax.fori_loop(2, 2 + reach, own, 0, unroll=6)
+    lax.fori_loop(2 + rows - reach, 2 + rows, own, 0, unroll=6)
     lax.fori_loop(rows + 2, rows + 4, functools.partial(second_velocity, False), 0, unroll=2)
+    for r in range(reach, rows - reach):
+        density[pl.ds(r, levels, stride=rows), :] = inner_density[r - reach]
+        for k in range(6):
+            x = inner_vel[k, r - reach]
+            vel[k, V_ROWS + r] = x
+            at = k % 3 * levels * rows + r
+            (fwd, adj)[k // 3][pl.ds(at, levels, stride=rows), :] = x[:, :cols]
+
+    split = 3 * levels * rows
+    early, late = pl.ds(0, split), pl.ds(split, 6 * levels * rows)
+    copies = [
+        pltpu.make_async_copy(fwd.at[early], fwd_out.at[early], sems.at[0]),
+        pltpu.make_async_copy(adj.at[early], adj_out.at[early], sems.at[1]),
+        pltpu.make_async_copy(density, density_out, sems.at[2]),
+    ]
+    for copy in copies:
+        copy.start()
 
     def second_stress(r, carry):
         i = r + S_ROWS
@@ -588,7 +655,15 @@
                 )
         return carry
 
-    lax.fori_loop(0, rows, second_stress, 0, unroll=4)
+    lax.fori_loop(0, rows, second_stress, 0, unroll=8)
+    copies += [
+        pltpu.make_async_copy(fwd.at[late], fwd_out.at[late], sems.at[3]),
+        pltpu.make_async_copy(adj.at[late], adj_out.at[late], sems.at[4]),
+    ]
+    for copy in copies[3:]:
+        copy.start()
+    for copy in copies:
+        copy.wait()
 
 
 def swap_tiles(x, first):
@@ -609,14 +684,14 @@
     return lax.ppermute(x, ("lon", "colat"), pairs)
 
 
-def call(kernel, out_shapes, specs, cost=0, limit=16 * 2**20, **more):
+def call(kernel, out_shapes, specs, cost=0, out=None, **more):
     return pl.pallas_call(
         kernel,
         out_shape=out_shapes,
         in_specs=specs,
-        out_specs=jax.tree.map(lambda _: vmem(), out_shapes),
+        out_specs=jax.tree.map(lambda _: out or vmem(), out_shapes),
         cost_estimate=pl.CostEstimate(flops=cost, bytes_accessed=cost, transcendentals=0),
-        compiler_params=pltpu.CompilerParams(vmem_limit_bytes=limit),
+        compiler_params=pltpu.CompilerParams(vmem_limit_bytes=16 * 2**20),
         **more,
     )
 
@@ -636,8 +711,9 @@
     def shape(*dims):
         return jax.ShapeDtypeStruct(dims, F32)
 
-    parts = forward_state, adjoint_state, layer_ids.astype(F32)
+    parts = forward_state, adjoint_state
     state = jnp.concatenate([x.reshape(-1, rows, cols) for x in parts]).reshape(-1, cols)
+    ids = layer_ids.reshape(levels * rows, cols)
 
     edges = shape(pieces(19 * rows, EDGE), levels, LANES)
     near = shape(len(NEAR), levels, cols)
@@ -645,11 +721,13 @@
     edge_a, edge_b, near_a, near_b, far_a, far_b = call(
         functools.partial(pack_kernel, dims),
         [edges, edges, near, near, far, far],
-        [vmem()],
+        [vmem()] * 2,
         cost=10**6,
-    )(state)
-    near_b, near_a = swap_bands(near_b, False), swap_bands(near_a, True)
-    edge_b, edge_a = swap_tiles(edge_b, False), swap_tiles(edge_a, True)
+    )(state, ids)
+    near_b = swap_bands(near_b, False)
+    near_a = swap_bands(near_a, True)
+    edge_b = swap_tiles(edge_b, False)
+    edge_a = swap_tiles(edge_a, True)
     far_b = swap_bands(far_b, False)
     far_a = swap_bands(far_a, True)
 
@@ -671,20 +749,19 @@
         cost=10**8,
     )(given)
 
-    extra = len(VEL + NEAR + FAR) + S_ROWS
-    payload = shape(len(VEL) * tiles + pieces(extra, 2 * EDGE), levels, LANES)
+    payload = shape(len(VEL) * tiles + side_plan()[1], levels, LANES)
     stress_shape = shape(12, rows + 2 * S_ROWS, levels, width)
     mats_shape = shape(3, rows + 2 * S_ROWS, levels, width)
     stress, vel, pay_a, pay_b = call(
         functools.partial(velocity_kernel, dims, consts),
         [stress_shape, shape(6, rows, levels, width), payload, payload],
-        [vmem()] * 8 + [smem()],
+        [vmem()] * 9 + [smem()],
         cost=10**7,
         scratch_shapes=[
             pltpu.VMEM((rows, levels, width), F32),
             pltpu.VMEM((rows, levels, LANES), F32),
         ],
-    )(state, edge_a, edge_b, near_a, near_b, ap, cv, first, density_table)
+    )(state, ids, edge_a, edge_b, near_a, near_b, ap, cv, first, density_table)
     got_b, got_a = swap_bands(pay_b, False), swap_bands(pay_a, True)
 
     second = call(
@@ -693,26 +770,39 @@
         [vmem()],
         cost=10**8,
     )(given)
-    halo, mats = call(
-        functools.partial(fill_kernel, dims, dt),
-        [shape(12, 2 * S_ROWS, levels, cols), mats_shape],
-        [vmem()] * 6 + [smem()] * 3,
+    halo, mats, inner_stress, inner_vel, inner_density = call(
+        functools.partial(fill_kernel, dims, consts),
+        [
+            shape(12, 2 * S_ROWS, levels, cols),
+            mats_shape,
+            shape(12, rows - 2 * INNER, levels, width),
+            shape(6, rows - 2 * INNER - 4, levels, width),
+            shape(rows - 2 * INNER - 4, levels, cols),
+        ],
+        [vmem()] * 10 + [smem()] * 3,
         cost=10**8,
-    )(stress, state, edge_a, edge_b, far_a, far_b, density_table, lame_table, shear_table)
-
+    )(
+        stress, vel, ids, edge_a, edge_b, far_a, far_b, second, ap, cv,
+        density_table, lame_table, shear_table,
+    )
+
+    flat = (9 * levels * rows, cols), (9 * levels * rows, cols), (levels * rows, cols)
     fwd, adj, density = call(
         functools.partial(final_kernel, dims, consts),
-        [shape(9 * levels * rows, cols)] * 2 + [shape(levels * rows, cols)],
-        [vmem()] * 9 + [smem()] * 3,
+        [shape(*x) for x in flat],
+        [vmem()] * 12 + [smem()] * 3,
         cost=10**8,
+        out=pl.BlockSpec(memory_space=pltpu.HBM),
         scratch_shapes=[
             pltpu.VMEM((6, rows + 2 * V_ROWS, levels, width), F32),
             pltpu.VMEM(stress_shape.shape, F32),
             pltpu.VMEM(mats_shape.shape, F32),
-        ],
+        ]
+        + [pltpu.VMEM(x, F32) for x in flat]
+        + [pltpu.SemaphoreType.DMA((5,))],
     )(
         vel, stress, halo, got_a, got_b, mats, second, ap, cv,
-        density_table, lame_table, shear_table,
+        inner_stress, inner_vel, inner_density, density_table, lame_table, shear_table,
     )
     return (
         fwd.reshape(forward_state.shape),

time: 40.9 us -> 37.8 us (0.924)
  Pallas kernels: 14.5 us -> 12.7 us
  other arithmetic: 2.19 us -> 1.37 us
  waiting for transfers between devices: 12 us -> 11.2 us
    ppermute x6, starting transfers between devices: 5.92 us -> 10.1 us  [swap_bands(): return lax.ppermute(x, ('lon', 'colat'), pairs)]
    ppermute x6, waiting for transfers between devices: 12 us -> 8.02 us  [swap_bands(): return lax.ppermute(x, ('lon', 'colat'), pairs)]
    ppermute x2, starting transfers between devices: 5.26 us -> 1.46 us  [swap_tiles(): return lax.ppermute(x, 'lon', list(to.items()))]
    ppermute x2, waiting for transfers between devices: 0.01 us -> 3.2 us  [swap_tiles(): return lax.ppermute(x, 'lon', list(to.items()))]
    pallas_call x1, Pallas kernels: 3.43 us -> 2.57 us  [on_device(): call(functools.partial(velocity_kernel, dims, consts), [stress_shape, sha...]
    convert_element_type x1 -> x0, other arithmetic: 0.85 us -> none  [on_device(): parts = (forward_state, adjoint_state, layer_ids.astype(F32))]
    pallas_call x2, Pallas kernels: 7.31 us -> 6.56 us  [the longest x1 4.66 us: on_device(): call(functools.partial(final_kernel, dims, consts), [shape(*x) for x in f...]
  transfers between devices with their start and end apart: 8 -> 8, of which waited for: 4 -> 3; matrix products, arithmetic and copies ran while one was open for 0% -> 0% of each run, Pallas kernels for 10% -> 13%
where the time goes in v1:
time: 37.8 us; the launch traced here: 37.7 us
  Pallas kernels  12.7 us (34%)
  starting transfers between devices  11.6 us (31%)
  waiting for transfers between devices  11.2 us (30%)
  other arithmetic  1.37 us (4%)
  between operations  0.79 us (2%)
    ppermute x6, starting transfers between devices, swap_bands(): return lax.ppermute(x, ('lon', 'colat'), pairs)  10.1 us
    ppermute x6, waiting for transfers between devices, swap_bands(): return lax.ppermute(x, ('lon', 'colat'), pairs)  8.02 us
    pallas_call x1, Pallas kernels, on_device(): call(functools.partial(final_kernel, dims, consts), [shape(*x) for x in f...  4.66 us
    ppermute x2, waiting for transfers between devices, swap_tiles(): return lax.ppermute(x, 'lon', list(to.items()))  3.2 us
    pallas_call x1, Pallas kernels, on_device(): call(functools.partial(velocity_kernel, dims, consts), [stress_shape, sha...  2.57 us
    pallas_call x1, Pallas kernels, on_device(): call(functools.partial(second_inject_kernel, dims, extents), shape(4, row...  2.14 us
    pallas_call x1, Pallas kernels, on_device(): call(functools.partial(fill_kernel, dims, consts), [shape(12, 2 * S_ROWS,...  1.9 us
    ppermute x2, starting transfers between devices, swap_tiles(): return lax.ppermute(x, 'lon', list(to.items()))  1.46 us
  transfers between devices with their start and end apart: 8, of which 3 were waited for; matrix products, arithmetic and copies ran while one was open for 0% of the time, Pallas kernels for 13%

profile of v1, /device:TPU:0, one launch (start us, length us, event | category | flops | bytes accessed | tf_op | source)
XLA Modules:
  0.0 37.7 jit_solution(1555467815068511265)
XLA Ops:
  0.6 0.0 copy-start
  0.6 1.4 %pad_maximum_fusion = f32[144,16,128]{2,1,0:T(8,128)S(1)} fusion(f32[72,16,128]{2,1,0:T(8,128)} %bitcast.15, f32[72,16,128]{2,1,0:T(8,128)} %bitcast.16), kind=kLoop, calls=%fused_computation | loop fusion | flops 294912 | bytes 2359296 | tf_op jit(solution)/shard_map/concatenate | solution.py:715
  2.0 0.0 copy-start.7
  2.0 0.0 copy-start.5
  2.0 0.0 copy-start.4
  2.0 0.0 copy-start.6
  2.0 0.0 copy-start.1
  2.1 0.0 copy-done
  2.1 0.5 %shard_map.121 = (f32[19,8,128]{2,1,0:T(8,128)S(1)}, f32[19,8,128]{2,1,0:T(8,128)S(1)}, f32[12,8,128]{2,1,0:T(8,128)S(1)}, f32[12,8,128]{2,1,0:T(8,128)S(1)}, f3...) custom-call(f32[2304,128]{1,0:T(8,128)S(1)} %bitcast.10, s32[128,128]{1,0:T(8,128)S(1)} %bitcast.12), custom_call_target="tpu_custom_call" | custom-call | flops 1000000 | bytes 1000000 | tf_op jit(solution)/shard_map/pallas_call | solution.py:721
  2.6 3.0 %collective-permute-start.2 = (f32[12,8,128]{2,1,0:T(8,128)S(1)}, f32[12,8,128]{2,1,0:T(8,128)S(1)}, u32[]{:S(2)}, u32[]{:S(2)}) collective-permute-start(f32[12,8,128]{2,1,0:T(8,128)S(1)} %get-tuple-element.26), channel_id=1, source_target_pairs={{0,1},{1,0},{2,3},{3,2},{4,5},{5,4},{6,7},{7,6},{8,9},{9,8},{10,11... | collective-permute-start | bytes 147464 | tf_op jit(solution)/shard_map/ppermute | solution.py:684
  5.6 2.6 %collective-permute-start.3 = (f32[12,8,128]{2,1,0:T(8,128)S(1)}, f32[12,8,128]{2,1,0:T(8,128)S(1)}, u32[]{:S(2)}, u32[]{:S(2)}) collective-permute-start(f32[12,8,128]{2,1,0:T(8,128)S(1)} %get-tuple-element.27), channel_id=1, source_target_pairs={{0,16},{1,2},{2,1},{3,19},{4,20},{5,6},{6,5},{7,23},{8,24},{9,10},... | collective-permute-start | bytes 147464 | tf_op jit(solution)/shard_map/ppermute | solution.py:684
  8.2 0.0 collective-permute-start
  8.2 1.5 %collective-permute-start.1 = (f32[19,8,128]{2,1,0:T(8,128)S(1)}, f32[19,8,128]{2,1,0:T(8,128)S(1)}, u32[]{:S(2)}, u32[]{:S(2)}) collective-permute-start(f32[19,8,128]{2,1,0:T(8,128)S(1)} %get-tuple-element.25), channel_id=1, source_target_pairs={{0,28},{4,8},{8,4},{12,16},{16,12},{20,24},{24,20},{28,0},{1,29},{... | collective-permute-start | bytes 233480 | tf_op jit(solution)/shard_map/ppermute | solution.py:672
  9.6 0.0 copy-done.7
  9.6 0.0 copy-done.5
  9.7 0.0 copy-done.4
  9.7 0.0 copy-done.6
  9.7 0.9 %shard_map.122 = (f32[4,16,8,256]{3,2,1,0:T(8,128)S(1)}, f32[24,8,128]{2,1,0:T(8,128)S(1)}, f32[24,8,128]{2,1,0:T(8,128)S(1)}) custom-call(f32[10,512]{1,0:T(8,128)S(1)} %select_maximum_fusion.given), custom_call_target="tpu_custom_call" | custom-call | flops 100000000 | bytes 100000000 | tf_op jit(solution)/shard_map/pallas_call | solution.py:745
  10.7 0.0 collective-permute-done.2.near_a
  10.7 0.0 collective-permute-done.3.near_b
  10.7 0.0 collective-permute-done.edge_a.id_edge_a
  10.7 3.2 %collective-permute-done.1.edge_b.id_edge_b = f32[19,8,128]{2,1,0:T(8,128)S(1)} collective-permute-done((f32[19,8,128]{2,1,0:T(8,128)S(1)}, f32[19,8,128]{2,1,0:T(8,128)S(1)}, u32[]{:S(2)}, u32[]{:S(2)}) %collective-permute-start.1) | collective-permute-done | bytes 77856 | tf_op jit(solution)/shard_map/ppermute | solution.py:672
  13.9 0.0 copy-done.1
  13.9 0.0 copy-start.2
  13.9 0.0 copy-start.3
  13.9 2.6 %shard_map.123 = (f32[12,24,8,256]{3,2,1,0:T(8,128)S(1)}, f32[6,16,8,256]{3,2,1,0:T(8,128)S(1)}, f32[42,8,128]{2,1,0:T(8,128)S(1)}, f32[42,8,128]{2,1,0:T(8,128)S(1)}) custom-call(f32[2304,128]{1,0:T(8,128)S(1)} %bitcast.11, s32[128,128]{1,0:T(8,128)S(1)} %bitcast.13, f32[19,8,128]{2,1,0:T(8,128)S(1)} %collective-permute-done.edge_a.id_edge_a, ...), custom_call_target="tpu_custom_call" | custom-call | flops 10000000 | bytes 10000000 | tf_op jit(solution)/shard_map/pallas_call | solution.py:755
  16.5 0.6 %collective-permute-start.6 = (f32[42,8,128]{2,1,0:T(8,128)S(1)}, f32[42,8,128]{2,1,0:T(8,128)S(1)}, u32[]{:S(2)}, u32[]{:S(2)}) collective-permute-start(f32[42,8,128]{2,1,0:T(8,128)S(1)} %get-tuple-element.36), channel_id=1, source_target_pairs={{0,1},{1,0},{2,3},{3,2},{4,5},{5,4},{6,7},{7,6},{8,9},{9,8},{10,11... | collective-permute-start | bytes 516104 | tf_op jit(solution)/shard_map/ppermute | solution.py:684
  17.1 0.5 %collective-permute-start.7 = (f32[42,8,128]{2,1,0:T(8,128)S(1)}, f32[42,8,128]{2,1,0:T(8,128)S(1)}, u32[]{:S(2)}, u32[]{:S(2)}) collective-permute-start(f32[42,8,128]{2,1,0:T(8,128)S(1)} %get-tuple-element.37), channel_id=1, source_target_pairs={{0,16},{1,2},{2,1},{3,19},{4,20},{5,6},{6,5},{7,23},{8,24},{9,10},... | collective-permute-start | bytes 516104 | tf_op jit(solution)/shard_map/ppermute | solution.py:684
  17.6 2.4 %collective-permute-start.4 = (f32[28,8,128]{2,1,0:T(8,128)S(1)}, f32[28,8,128]{2,1,0:T(8,128)S(1)}, u32[]{:S(2)}, u32[]{:S(2)}) collective-permute-start(f32[28,8,128]{2,1,0:T(8,128)S(1)} %get-tuple-element.33), channel_id=1, source_target_pairs={{0,1},{1,0},{2,3},{3,2},{4,5},{5,4},{6,7},{7,6},{8,9},{9,8},{10,11... | collective-permute-start | bytes 344072 | tf_op jit(solution)/shard_map/ppermute | solution.py:684
  20.1 0.9 %collective-permute-start.5 = (f32[28,8,128]{2,1,0:T(8,128)S(1)}, f32[28,8,128]{2,1,0:T(8,128)S(1)}, u32[]{:S(2)}, u32[]{:S(2)}) collective-permute-start(f32[28,8,128]{2,1,0:T(8,128)S(1)} %get-tuple-element.34), channel_id=1, source_target_pairs={{0,16},{1,2},{2,1},{3,19},{4,20},{5,6},{6,5},{7,23},{8,24},{9,10},... | collective-permute-start | bytes 344072 | tf_op jit(solution)/shard_map/ppermute | solution.py:684
  21.0 2.1 %shard_map.124.second = f32[4,20,8,256]{3,2,1,0:T(8,128)S(1)} custom-call(f32[10,512]{1,0:T(8,128)S(1)} %select_maximum_fusion.given), custom_call_target="tpu_custom_call" | custom-call | flops 100000000 | bytes 100000000 | tf_op jit(solution)/shard_map/pallas_call | solution.py:767
  23.1 5.7 %collective-permute-done.4.far_a = f32[28,8,128]{2,1,0:T(8,128)S(1)} collective-permute-done((f32[28,8,128]{2,1,0:T(8,128)S(1)}, f32[28,8,128]{2,1,0:T(8,128)S(1)}, u32[]{:S(2)}, u32[]{:S(2)}) %collective-permute-start.4) | collective-permute-done | bytes 114720 | tf_op jit(solution)/shard_map/ppermute | solution.py:684
  28.8 2.3 %collective-permute-done.5.far_b = f32[28,8,128]{2,1,0:T(8,128)S(1)} collective-permute-done((f32[28,8,128]{2,1,0:T(8,128)S(1)}, f32[28,8,128]{2,1,0:T(8,128)S(1)}, u32[]{:S(2)}, u32[]{:S(2)}) %collective-permute-start.5) | collective-permute-done | bytes 114720 | tf_op jit(solution)/shard_map/ppermute | solution.py:684
  31.1 0.0 copy-done.2
  31.1 0.0 copy-done.3
  31.1 1.9 %shard_map.125 = (f32[12,8,8,128]{3,2,1,0:T(8,128)S(1)}, f32[3,24,8,256]{3,2,1,0:T(8,128)S(1)}, f32[12,8,8,256]{3,2,1,0:T(8,128)S(1)}, f32[6,4,8,256]{3,2,1,0:T(8,128)S(1)}, f32[4,8,128]{2,1,0:T(8,128)S(1)}) custom-call(f32[12,24,8,256]{3,2,1,0:T(8,128)S(1)} %get-tuple-element.32.stress.stress_in, f32[6,16,8,256]{3,2,1,0:T(8,128)S(1)} %get-tuple-element.31.vel.vel_in, ...), custom_call_target="tpu_custom_call" | custom-call | flops 100000000 | bytes 100000000 | tf_op jit(solution)/shard_map/pallas_call | solution.py:773
  33.0 0.0 collective-permute-done.6.got_a
  33.0 0.0 collective-permute-done.7.got_b
  33.0 4.7 %shard_map.126 = (f32[1152,128]{1,0:T(8,128)}, f32[1152,128]{1,0:T(8,128)}, f32[128,128]{1,0:T(8,128)}) custom-call(f32[6,16,8,256]{3,2,1,0:T(8,128)S(1)} %get-tuple-element.31.vel.vel_in, f32[12,24,8,256]{3,2,1,0:T(8,128)S(1)} %get-tuple-element.32.stress.stress_in, f32[12,8,8,128]{3,2,1,0:T(8,128)S(1)} %get-tuple-element.35.halo, ...), custom_call_target="tpu_custom_call" | custom-call | flops 100000000 | bytes 100000000 | tf_op jit(solution)/shard_map/pallas_call | solution.py:790
  (5 shorter events, 0.0 us)
Async XLA Ops:
  0.6 1.4 %copy-start = (s32[8,16,128]{2,1,0:T(8,128)S(1)}, s32[8,16,128]{2,1,0:T(8,128)}, u32[]{:S(2)}) copy-start(s32[8,16,128]{2,1,0:T(8,128)} %param.12) | copy-start | bytes 196612
  2.0 7.6 %copy-start.7 = (s32[8]{0:T(128)S(1)}, s32[8]{0:T(128)}, u32[]{:S(2)}) copy-start(s32[8]{0:T(128)} %param.16) | copy-start | bytes 100
  2.0 7.6 %copy-start.5 = (s32[512]{0:T(512)S(1)}, s32[512]{0:T(512)}, u32[]{:S(2)}) copy-start(s32[512]{0:T(512)} %param.18) | copy-start | bytes 6148
  2.0 7.6 %copy-start.4 = (f32[2,3,512]{2,0,1:T(2,128)S(1)}, f32[2,3,512]{2,0,1:T(2,128)}, u32[]{:S(2)}) copy-start(f32[2,3,512]{2,0,1:T(2,128)} %param.19) | copy-start | bytes 36868
  2.0 7.7 %copy-start.6 = (f32[2,8]{1,0:T(2,128)S(1)}, f32[2,8]{1,0:T(2,128)}, u32[]{:S(2)}) copy-start(f32[2,8]{1,0:T(2,128)} %param.17) | copy-start | bytes 196
  2.0 11.9 %copy-start.1 = (f32[16]{0:T(128)S(1)}, f32[16]{0:T(128)}, u32[]{:S(2)}) copy-start(f32[16]{0:T(128)} %density_t.1) | copy-start | bytes 196
  2.6 8.1 %collective-permute-start.2 = (f32[12,8,128]{2,1,0:T(8,128)S(1)}, f32[12,8,128]{2,1,0:T(8,128)S(1)}, u32[]{:S(2)}, u32[]{:S(2)}) collective-permute-start(f32[12,8,128]{2,1,0:T(8,128)S(1)} %get-tuple-element.26), channel_id=1, source_target_pairs={{0,1},{1,0},{2,3},{3,2},{4,5},{5,4},{6,7},{7,6},{8,9},{9,8},{10,11... | collective-permute-start | bytes 147464 | tf_op jit(solution)/shard_map/ppermute | solution.py:684
  5.6 5.1 %collective-permute-start.3 = (f32[12,8,128]{2,1,0:T(8,128)S(1)}, f32[12,8,128]{2,1,0:T(8,128)S(1)}, u32[]{:S(2)}, u32[]{:S(2)}) collective-permute-start(f32[12,8,128]{2,1,0:T(8,128)S(1)} %get-tuple-element.27), channel_id=1, source_target_pairs={{0,16},{1,2},{2,1},{3,19},{4,20},{5,6},{6,5},{7,23},{8,24},{9,10},... | collective-permute-start | bytes 147464 | tf_op jit(solution)/shard_map/ppermute | solution.py:684
  8.2 2.5 %collective-permute-start = (f32[19,8,128]{2,1,0:T(8,128)S(1)}, f32[19,8,128]{2,1,0:T(8,128)S(1)}, u32[]{:S(2)}, u32[]{:S(2)}) collective-permute-start(f32[19,8,128]{2,1,0:T(8,128)S(1)} %get-tuple-element.24), channel_id=1, source_target_pairs={{0,4},{4,0},{8,12},{12,8},{16,20},{20,16},{24,28},{28,24},{1,5},{5... | collective-permute-start | bytes 233480 | tf_op jit(solution)/shard_map/ppermute | solution.py:672
  8.2 5.7 %collective-permute-start.1 = (f32[19,8,128]{2,1,0:T(8,128)S(1)}, f32[19,8,128]{2,1,0:T(8,128)S(1)}, u32[]{:S(2)}, u32[]{:S(2)}) collective-permute-start(f32[19,8,128]{2,1,0:T(8,128)S(1)} %get-tuple-element.25), channel_id=1, source_target_pairs={{0,28},{4,8},{8,4},{12,16},{16,12},{20,24},{24,20},{28,0},{1,29},{... | collective-permute-start | bytes 233480 | tf_op jit(solution)/shard_map/ppermute | solution.py:672
  13.9 17.2 %copy-start.2 = (f32[16]{0:T(128)S(1)}, f32[16]{0:T(128)}, u32[]{:S(2)}) copy-start(f32[16]{0:T(128)} %lame_t.1) | copy-start | bytes 196
  13.9 17.2 %copy-start.3 = (f32[16]{0:T(128)S(1)}, f32[16]{0:T(128)}, u32[]{:S(2)}) copy-start(f32[16]{0:T(128)} %shear_t.1) | copy-start | bytes 196
  16.5 16.5 %collective-permute-start.6 = (f32[42,8,128]{2,1,0:T(8,128)S(1)}, f32[42,8,128]{2,1,0:T(8,128)S(1)}, u32[]{:S(2)}, u32[]{:S(2)}) collective-permute-start(f32[42,8,128]{2,1,0:T(8,128)S(1)} %get-tuple-element.36), channel_id=1, source_target_pairs={{0,1},{1,0},{2,3},{3,2},{4,5},{5,4},{6,7},{7,6},{8,9},{9,8},{10,11... | collective-permute-start | bytes 516104 | tf_op jit(solution)/shard_map/ppermute | solution.py:684
  17.1 15.9 %collective-permute-start.7 = (f32[42,8,128]{2,1,0:T(8,128)S(1)}, f32[42,8,128]{2,1,0:T(8,128)S(1)}, u32[]{:S(2)}, u32[]{:S(2)}) collective-permute-start(f32[42,8,128]{2,1,0:T(8,128)S(1)} %get-tuple-element.37), channel_id=1, source_target_pairs={{0,16},{1,2},{2,1},{3,19},{4,20},{5,6},{6,5},{7,23},{8,24},{9,10},... | collective-permute-start | bytes 516104 | tf_op jit(solution)/shard_map/ppermute | solution.py:684
  17.6 11.2 %collective-permute-start.4 = (f32[28,8,128]{2,1,0:T(8,128)S(1)}, f32[28,8,128]{2,1,0:T(8,128)S(1)}, u32[]{:S(2)}, u32[]{:S(2)}) collective-permute-start(f32[28,8,128]{2,1,0:T(8,128)S(1)} %get-tuple-element.33), channel_id=1, source_target_pairs={{0,1},{1,0},{2,3},{3,2},{4,5},{5,4},{6,7},{7,6},{8,9},{9,8},{10,11... | collective-permute-start | bytes 344072 | tf_op jit(solution)/shard_map/ppermute | solution.py:684
  20.1 11.0 %collective-permute-start.5 = (f32[28,8,128]{2,1,0:T(8,128)S(1)}, f32[28,8,128]{2,1,0:T(8,128)S(1)}, u32[]{:S(2)}, u32[]{:S(2)}) collective-permute-start(f32[28,8,128]{2,1,0:T(8,128)S(1)} %get-tuple-element.34), channel_id=1, source_target_pairs={{0,16},{1,2},{2,1},{3,19},{4,20},{5,6},{6,5},{7,23},{8,24},{9,10},... | collective-permute-start | bytes 344072 | tf_op jit(solution)/shard_map/ppermute | solution.py:684

commit v2 on v1

--- a/solution.py
+++ b/solution.py
@@ -148,11 +148,11 @@
     return q, x - q * by
 
 
-def inject(dims, extents, step, given, out, halo):
+def inject_kernel(dims, extents, given, first, second):
     levels, rows, cols = dims
     lat_cells, lon_cells = extents
     width = cols + LANES
-    north_sign, south_sign = pole_signs()
+    signs = (1.0,) + pole_signs()
     first_row, first_col = lax.axis_index("colat") * rows, lax.axis_index("lon") * cols
     at_top, at_bottom = first_row == 0, first_row + rows == lat_cells
     half = lon_cells // 2
@@ -173,68 +173,67 @@
             inside = jnp.logical_and(r >= 0, r < count)
             return jnp.where(inside, r * levels + level, -1)
 
-        north = 1 - jnp.where(at_top, row, first_row - 1 - row)
+        north = V_ROWS - 1 - jnp.where(at_top, row, first_row - 1 - row)
         south = jnp.where(at_bottom, lat_cells - 1 - row, row - first_row - rows)
         return (
             (code(row - first_row, rows), lane(col)),
-            (code(north, 2), lane(jnp.where(at_top, col + half, col))),
-            (code(south, 2), lane(jnp.where(at_bottom, col + half, col))),
+            (code(north, V_ROWS), lane(jnp.where(at_top, col + half, col))),
+            (code(south, V_ROWS), lane(jnp.where(at_bottom, col + half, col))),
         )
 
-    def spread(place, value_rows, count):
-        code, lane = place
-        n = code.shape[1]
-        hot_rows = lax.broadcasted_iota(jnp.int32, (count * levels, n), 0) == code
-        hot = lax.broadcasted_iota(jnp.int32, (width, n), 0) == lane
-        hot = jnp.where(hot, 1.0, 0.0).astype(jnp.bfloat16)
-        out = []
-        for value in value_rows:
-            rest = jnp.where(hot_rows, value, 0.0)
-            total = None
-            for _ in range(3):
-                part = rest.astype(jnp.bfloat16)
-                rest = rest - part.astype(F32)
-                term = lax.dot_general(
-                    part, hot, (((1,), (1,)), ((), ())), preferred_element_type=F32
-                )
-                total = term if total is None else total + term
-            out.append(total.reshape(count, levels, width))
+    def parts(value):
+        out, rest = [], value
+        for _ in range(3):
+            part = rest.astype(jnp.bfloat16)
+            out.append(part)
+            rest = rest - part.astype(F32)
         return out
 
-    places = located(given[0:1, :].astype(jnp.int32))
-    splaces = located(given[7:8, :LANES].astype(jnp.int32))
-    values = [given[1 + 3 * step + c : 2 + 3 * step + c, :] for c in range(3)]
-    svalues = [given[8 + step : 9 + step, :LANES]]
-    regions = ((0, halo, rows, 1.0), (1, 0, halo, north_sign), (2, halo + rows, halo, south_sign))
-    for where, at, count, sign in regions:
-        if count:
-            out[0, at : at + count] = spread(splaces[where], svalues, count)[0]
-            for c, got in enumerate(spread(places[where], values, count)):
-                signed = where and FIELD_SIGNS[c] < 0
-                out[1 + c, at : at + count] = got * sign if signed else got
-
-
-def first_inject_kernel(dims, extents, given, out, ap, cv):
+    def hot(ids, size):
+        same = lax.broadcasted_iota(jnp.int32, (size, ids.shape[1]), 0) == ids
+        return jnp.where(same, 1.0, 0.0).astype(jnp.bfloat16)
+
+    def line(n, size):
+        return given[n : n + 1, :size]
+
+    places = located(line(0, None).astype(jnp.int32))
+    splaces = located(line(7, LANES).astype(jnp.int32))
+    regions = ((V_ROWS, rows), (0, V_ROWS), (V_ROWS + rows, V_ROWS))
+    receivers = [(s, 1 + c, parts(line(1 + 3 * s + c, None))) for s in range(2) for c in range(3)]
+    sources = [(s, 0, parts(line(8 + s, LANES))) for s in range(2)]
+    for n, (at, count) in enumerate(regions):
+        size = count * levels
+        for place, todo in ((places[n], receivers), (splaces[n], sources)):
+            on_row, on_lane = hot(place[0], size), hot(place[1], width)
+            stacked = jnp.concatenate([on_row * part for _, _, three in todo for part in three])
+            spread = lax.dot_general(
+                stacked, on_lane, (((1,), (1,)), ((), ())), preferred_element_type=F32
+            )
+            for m, (s, k, _) in enumerate(todo):
+                rest = [spread[(3 * m + p) * size : (3 * m + p + 1) * size] for p in range(3)]
+                total = rest[0] + rest[1] + rest[2]
+                if n and k and FIELD_SIGNS[k - 1] < 0:
+                    total = total * signs[n]
+                (first, second)[s][k, at : at + count] = total.reshape(count, levels, width)
+
+
+def geometry(dims, extents):
     levels, rows, _ = dims
     lat_cells, lon_cells = extents
     first_row = lax.axis_index("colat") * rows
-    inject(dims, extents, 0, given, out, 0)
-    deep = rows + 2 * S_ROWS
-    g = lax.broadcasted_iota(jnp.int32, (deep, LANES), 0) + (first_row - S_ROWS)
+    g = first_row + jnp.arange(-S_ROWS, rows + S_ROWS, dtype=jnp.int32)
     sign = jnp.where(jnp.logical_or(g < 0, g >= lat_cells), -1.0, 1.0)
     g = jnp.where(g < 0, -1 - g, jnp.where(g >= lat_cells, 2 * lat_cells - 1 - g, g))
     angle = (g.astype(F32) + 0.5) * (math.pi / lat_cells)
     held = jnp.maximum(jnp.sin(angle), SIN_FLOOR)
-    across = sign / (held * (24.0 * math.pi / lon_cells))
-    cot = sign * jnp.cos(angle) / held
-    ir = level_vectors(levels, LANES, (1.0 - R_INNER) / levels, math.pi / lat_cells)[0]
-    for i in range(deep):
-        ap[i] = ir * across[i : i + 1, :]
-        cv[i] = ir * cot[i : i + 1, :]
-
-
-def second_inject_kernel(dims, extents, given, out):
-    inject(dims, extents, 1, given, out, 2)
+    pair = sign / (held * (24.0 * math.pi / lon_cells)), sign * jnp.cos(angle) / held
+    pair = lax.optimization_barrier(pair)
+    k = jnp.arange(levels, dtype=F32)
+    ir = 1.0 / (R_INNER + (k + 0.5) * ((1.0 - R_INNER) / levels))
+    shape = g.shape[0], levels, LANES
+    return tuple(
+        jnp.broadcast_to(x[:, None, None] * ir[None, :, None], shape) for x in pair
+    )
 
 
 def level_vectors(levels, width, dr, theta_step):
@@ -340,14 +339,12 @@
 
 
 def velocity_kernel(
-    dims, consts, state, ids, edge_a, edge_b, near_a, near_b, ap, cv, first, density,
-    stress, vel, pay_a, pay_b, rho, id_side,
+    dims, consts, state, ids, edge_a, edge_b, near_a, near_b, ap, cv, given, density,
+    stress, vel, rho, id_side, pay_b,
 ):
     levels, rows, cols = dims
-    dr, theta_step, dt = consts
-    width = cols + LANES
+    _, _, dt = consts
     signs = pole_signs()
-    even = even_band()
     per = LANES // EDGE
     paired = {}
 
@@ -382,6 +379,28 @@
             stress[f * 6 + c - 3, i, :, :cols] = main
             stress[f * 6 + c - 3, i, :, cols:] = jnp.zeros((levels, LANES), F32)
 
+    base = jnp.where(even_band(), 0, rows - V_ROWS)
+    step = velocity_step(dims, consts, stress, vel, vel, rho, ap, cv)
+    lax.fori_loop(0, V_ROWS, lambda q, carry: step(base + q, carry), 0, unroll=V_ROWS)
+    payload(dims, jnp.logical_not(even_band()), stress, vel, id_side, pay_b)
+
+
+def rest_kernel(dims, consts, stress, vel_in, rho, id_side, ap, cv, vel, pay_a):
+    _, rows, _ = dims
+    done = jnp.where(even_band(), 0, rows - V_ROWS)
+    base = jnp.where(even_band(), V_ROWS, 0)
+    for q in range(V_ROWS):
+        for k in range(6):
+            vel[k, done + q] = vel_in[k, done + q]
+    step = velocity_step(dims, consts, stress, vel_in, vel, rho, ap, cv)
+    lax.fori_loop(0, rows - V_ROWS, lambda q, carry: step(base + q, carry), 0, unroll=5)
+    payload(dims, even_band(), stress, vel, id_side, pay_a)
+
+
+def velocity_step(dims, consts, stress, before, after, rho, ap, cv):
+    levels, _, cols = dims
+    dr, theta_step, _ = consts
+    width = cols + LANES
     vectors = level_vectors(levels, width, dr, theta_step)
 
     def step(r, carry):
@@ -390,42 +409,41 @@
         row_ap, row_cv = widened(ap[i], width), widened(cv[i], width)
         for f in range(2):
             for c, force in enumerate(forces(stress, f, i, vectors, row_ap, row_cv)):
-                new = vel[f * 3 + c, r] + scale * force
-                if f == 1 or c == 2:
-                    new = new + first[f * (1 + c), r]
-                vel[f * 3 + c, r] = new
+                after[f * 3 + c, r] = before[f * 3 + c, r] + scale * force
         return carry
 
-    lax.fori_loop(0, rows, step, 0, unroll=8)
-
+    return step
+
+
+def payload(dims, bottom_side, stress, vel, id_side, ref):
+    levels, rows, cols = dims
     tiles = cols // LANES
     plan, vectors_out = side_plan()
-    for ref, bottom_side in ((pay_a, even), (pay_b, jnp.logical_not(even))):
-
-        def facing(d):
-            return jnp.where(bottom_side, rows - d, d - 1)
-
-        for k, (f, c, d) in enumerate(VEL):
-            for t in range(tiles):
-                at = slice(t * LANES, (t + 1) * LANES)
-                ref[k * tiles + t] = vel[f * 3 + c, facing(d), :, at]
-        packed, lanes = [None] * vectors_out, lane_iota((levels, LANES))
-        for (kind, f, c, d), (v, lane, wide) in plan.items():
-            if kind == "v":
-                x = vel[f * 3 + c, facing(d), :, cols:]
-            elif kind == "s":
-                x = stress[f * 6 + c - 3, facing(d) + S_ROWS, :, cols:]
-            else:
-                x = id_side[facing(d)]
-            x = rolled(x, lane + wide // 2)
-            packed[v] = x if packed[v] is None else jnp.where(lanes >= lane, x, packed[v])
-        for v, x in enumerate(packed):
-            ref[len(VEL) * tiles + v] = x
+
+    def facing(d):
+        return jnp.where(bottom_side, rows - d, d - 1)
+
+    for k, (f, c, d) in enumerate(VEL):
+        for t in range(tiles):
+            at = slice(t * LANES, (t + 1) * LANES)
+            ref[k * tiles + t] = vel[f * 3 + c, facing(d), :, at]
+    packed, lanes = [None] * vectors_out, lane_iota((levels, LANES))
+    for (kind, f, c, d), (v, lane, wide) in plan.items():
+        if kind == "v":
+            x = vel[f * 3 + c, facing(d), :, cols:]
+        elif kind == "s":
+            x = stress[f * 6 + c - 3, facing(d) + S_ROWS, :, cols:]
+        else:
+            x = id_side[facing(d)]
+        x = rolled(x, lane + wide // 2)
+        packed[v] = x if packed[v] is None else jnp.where(lanes >= lane, x, packed[v])
+    for v, x in enumerate(packed):
+        ref[len(VEL) * tiles + v] = x
 
 
 def fill_kernel(
-    dims, consts, stress, vel, ids, id_edge_a, id_edge_b, far_a, far_b, second, ap, cv,
-    density, lame, shear, halo, mats, inner_stress, inner_vel, inner_density,
+    dims, consts, stress, vel_in, ids, id_edge_a, id_edge_b, far_a, far_b, first, second, ap, cv,
+    density, lame, shear, halo, mats, vel, inner_stress, inner_vel, inner_density,
 ):
     levels, rows, cols = dims
     dr, theta_step, dt = consts
@@ -435,6 +453,13 @@
     per = LANES // EDGE
     paired = {}
 
+    for f in range(2):
+        for c in range(3):
+            for r in range(rows):
+                x = vel_in[f * 3 + c, r]
+                if f == 1 or c == 2:
+                    x = x + first[f * (1 + c), V_ROWS + r]
+                vel[f * 3 + c, r] = x
     for k, (f, c, d) in enumerate(FAR):
         for main, i, sign in zip(
             north_south(far_a, far_b, k), (S_ROWS - d, S_ROWS - 1 + d), signs
@@ -485,7 +510,7 @@
             for c, force in enumerate(steps):
                 new = vel[f * 3 + c, r] + mats[0, i] * force
                 if f == 1 or c == 2:
-                    new = new + second[f * (1 + c), r + 2]
+                    new = new + second[f * (1 + c), V_ROWS + r]
                 inner_vel[f * 3 + c, at] = new
                 fresh.append(new[:, :cols])
         products += [fresh[c] * fresh[3 + c] for c in range(3)]
@@ -496,7 +521,7 @@
 
 
 def final_kernel(
-    dims, consts, vel_in, stress_in, halo, got_a, got_b, mats_in, second, ap, cv,
+    dims, consts, vel_in, stress_in, halo, got_a, got_b, mats_in, first, second, ap, cv,
     inner_stress, inner_vel, inner_density, density_t, lame_t, shear_t,
     fwd_out, adj_out, density_out, vel, stress, mats, fwd, adj, density, sems,
 ):
@@ -516,16 +541,20 @@
         got = north_south(got_a, got_b, len(VEL) * tiles + v)
         return tuple(rolled(x, -lane - wide // 2) for x in got)
 
+    def put_velocity(f, c, d, at, values):
+        for x, i, sign in zip(values, (V_ROWS - d, V_ROWS + rows - 1 + d), signs):
+            if FIELD_SIGNS[c] < 0:
+                x = x * sign
+            if f == 1 or c == 2:
+                x = x + first[f * (1 + c), i, :, at]
+            vel[f * 3 + c, i, :, at] = x
+
     for k, (f, c, d) in enumerate(VEL):
-        flip = FIELD_SIGNS[c] < 0
         for t in range(tiles):
             at = slice(t * LANES, (t + 1) * LANES)
             north, south = north_south(got_a, got_b, k * tiles + t)
-            vel[f * 3 + c, V_ROWS - d, :, at] = north * signs[0] if flip else north
-            vel[f * 3 + c, V_ROWS + rows - 1 + d, :, at] = south * signs[1] if flip else south
-        at = V_ROWS - d, V_ROWS + rows - 1 + d
-        for x, i, sign in zip(sides("v", f, c, d), at, signs):
-            vel[f * 3 + c, i, :, side_at] = x * sign if flip else x
+            put_velocity(f, c, d, at, (north, south))
+        put_velocity(f, c, d, side_at, sides("v", f, c, d))
     for f, c, d in NEAR + FAR:
         n = f * 6 + c - 3
         for x, i, i_main, sign in zip(
@@ -605,7 +634,7 @@
             for c, force in enumerate(forces(stress, f, i, vectors, row_ap, row_cv)):
                 new = vel[f * 3 + c, j] + scale * force
                 if f == 1 or c == 2:
-                    new = new + second[f * (1 + c), r]
+                    new = new + second[f * (1 + c), j]
                 vel[f * 3 + c, j] = new
                 fresh.append(new[:, :cols])
         if own:
@@ -718,6 +747,7 @@
     edges = shape(pieces(19 * rows, EDGE), levels, LANES)
     near = shape(len(NEAR), levels, cols)
     far = shape(len(FAR) + S_ROWS, levels, cols)
+    extents = lat_cells, lon_cells
     edge_a, edge_b, near_a, near_b, far_a, far_b = call(
         functools.partial(pack_kernel, dims),
         [edges, edges, near, near, far, far],
@@ -731,7 +761,7 @@
     far_b = swap_bands(far_b, False)
     far_a = swap_bands(far_a, True)
 
-    deep = shape(rows + 2 * S_ROWS, levels, LANES)
+    ap, cv = geometry(dims, extents)
     count = max(LANES, receiver_cells.shape[0])
 
     def lines(x):
@@ -741,48 +771,42 @@
     given = jnp.concatenate(
         [lines(x) for x in (receiver_cells, receiver_residual, source_cells, source_wavelet)]
     )
-    extents = lat_cells, lon_cells
-    first, ap, cv = call(
-        functools.partial(first_inject_kernel, dims, extents),
-        [shape(4, rows, levels, width), deep, deep],
+    leaving = shape(len(VEL) * tiles + side_plan()[1], levels, LANES)
+    stress_shape = shape(12, rows + 2 * S_ROWS, levels, width)
+    mats_shape = shape(3, rows + 2 * S_ROWS, levels, width)
+    vel_shape = shape(6, rows, levels, width)
+    stress, vel, rho, id_side, pay_b = call(
+        functools.partial(velocity_kernel, dims, consts),
+        [stress_shape, vel_shape, shape(rows, levels, width), shape(rows, levels, LANES), leaving],
+        [vmem()] * 9 + [smem()],
+        cost=10**7,
+    )(state, ids, edge_a, edge_b, near_a, near_b, ap, cv, given, density_table)
+    got_b = swap_bands(pay_b, False)
+    vel, pay_a = call(
+        functools.partial(rest_kernel, dims, consts), [vel_shape, leaving], [vmem()] * 6, cost=10**7
+    )(stress, vel, rho, id_side, ap, cv)
+    got_a = swap_bands(pay_a, True)
+
+    first, second = call(
+        functools.partial(inject_kernel, dims, extents),
+        [shape(4, rows + 2 * V_ROWS, levels, width)] * 2,
         [vmem()],
         cost=10**8,
     )(given)
-
-    payload = shape(len(VEL) * tiles + side_plan()[1], levels, LANES)
-    stress_shape = shape(12, rows + 2 * S_ROWS, levels, width)
-    mats_shape = shape(3, rows + 2 * S_ROWS, levels, width)
-    stress, vel, pay_a, pay_b = call(
-        functools.partial(velocity_kernel, dims, consts),
-        [stress_shape, shape(6, rows, levels, width), payload, payload],
-        [vmem()] * 9 + [smem()],
-        cost=10**7,
-        scratch_shapes=[
-            pltpu.VMEM((rows, levels, width), F32),
-            pltpu.VMEM((rows, levels, LANES), F32),
-        ],
-    )(state, ids, edge_a, edge_b, near_a, near_b, ap, cv, first, density_table)
-    got_b, got_a = swap_bands(pay_b, False), swap_bands(pay_a, True)
-
-    second = call(
-        functools.partial(second_inject_kernel, dims, extents),
-        shape(4, rows + 4, levels, width),
-        [vmem()],
-        cost=10**8,
-    )(given)
-    halo, mats, inner_stress, inner_vel, inner_density = call(
+    halo, mats, full_vel, inner_stress, inner_vel, inner_density = call(
         functools.partial(fill_kernel, dims, consts),
         [
             shape(12, 2 * S_ROWS, levels, cols),
             mats_shape,
+            vel_shape,
             shape(12, rows - 2 * INNER, levels, width),
             shape(6, rows - 2 * INNER - 4, levels, width),
             shape(rows - 2 * INNER - 4, levels, cols),
         ],
-        [vmem()] * 10 + [smem()] * 3,
+        [vmem()] * 11 + [smem()] * 3,
         cost=10**8,
     )(
-        stress, vel, ids, edge_a, edge_b, far_a, far_b, second, ap, cv,
+        stress, vel, ids, edge_a, edge_b, far_a, far_b, first, second, ap, cv,
         density_table, lame_table, shear_table,
     )
 
@@ -790,7 +814,7 @@
     fwd, adj, density = call(
         functools.partial(final_kernel, dims, consts),
         [shape(*x) for x in flat],
-        [vmem()] * 12 + [smem()] * 3,
+        [vmem()] * 13 + [smem()] * 3,
         cost=10**8,
         out=pl.BlockSpec(memory_space=pltpu.HBM),
         scratch_shapes=[
@@ -801,7 +825,7 @@
         + [pltpu.VMEM(x, F32) for x in flat]
         + [pltpu.SemaphoreType.DMA((5,))],
     )(
-        vel, stress, halo, got_a, got_b, mats, second, ap, cv,
+        full_vel, stress, halo, got_a, got_b, mats, first, second, ap, cv,
         inner_stress, inner_vel, inner_density, density_table, lame_table, shear_table,
     )
     return (

time: 37.8 us -> 38.3 us (1.013)
  waiting for transfers between devices: 11.2 us -> 12.7 us
  Pallas kernels: 12.7 us -> 11.3 us
    pallas_call x3, Pallas kernels: 5.62 us -> 4.15 us  [the longest x1 1.84 us: on_device(): call(functools.partial(velocity_kernel, dims, consts), [stress_shape, vel...]
    ppermute x6, waiting for transfers between devices: 8.02 us -> 9.45 us  [swap_bands(): return lax.ppermute(x, ('lon', 'colat'), pairs)]
  transfers between devices with their start and end apart: 8 -> 8, of which waited for: 3 -> 4; matrix products, arithmetic and copies ran while one was open for 0% -> 0% of each run, Pallas kernels for 13% -> 9%
where the time goes in v2:
time: 38.3 us; the launch traced here: 38.2 us
  waiting for transfers between devices  12.7 us (33%)
  starting transfers between devices  11.6 us (30%)
  Pallas kernels  11.3 us (30%)
  other arithmetic  1.51 us (4%)
  between operations  0.85 us (2%)
    ppermute x6, starting transfers between devices, swap_bands(): return lax.ppermute(x, ('lon', 'colat'), pairs)  10.1 us
    ppermute x6, waiting for transfers between devices, swap_bands(): return lax.ppermute(x, ('lon', 'colat'), pairs)  9.45 us
    pallas_call x1, Pallas kernels, on_device(): call(functools.partial(final_kernel, dims, consts), [shape(*x) for x in f...  4.73 us
    ppermute x2, waiting for transfers between devices, swap_tiles(): return lax.ppermute(x, 'lon', list(to.items()))  3.2 us
    pallas_call x1, Pallas kernels, on_device(): call(functools.partial(fill_kernel, dims, consts), [shape(12, 2 * S_ROWS,...  1.98 us
    pallas_call x1, Pallas kernels, on_device(): call(functools.partial(velocity_kernel, dims, consts), [stress_shape, vel...  1.84 us
    ppermute x2, starting transfers between devices, swap_tiles(): return lax.ppermute(x, 'lon', list(to.items()))  1.46 us
    pallas_call x1, Pallas kernels, on_device(): call(functools.partial(inject_kernel, dims, extents), [shape(4, rows + 2...  1.46 us
  transfers between devices with their start and end apart: 8, of which 4 were waited for; matrix products, arithmetic and copies ran while one was open for 0% of the time, Pallas kernels for 9%

profile of v2, /device:TPU:0, one launch (start us, length us, event | category | flops | bytes accessed | tf_op | source)
XLA Modules:
  0.0 38.2 jit_solution(13477818816927216040)
XLA Ops:
  0.6 0.0 copy-start
  0.6 1.4 %pad_maximum_fusion = f32[144,16,128]{2,1,0:T(8,128)S(1)} fusion(f32[72,16,128]{2,1,0:T(8,128)} %bitcast.15, f32[72,16,128]{2,1,0:T(8,128)} %bitcast.16), kind=kLoop, calls=%fused_computation | loop fusion | flops 294912 | bytes 2359296 | tf_op jit(solution)/shard_map/concatenate | solution.py:744
  2.0 0.0 copy-start.7
  2.0 0.0 copy-start.5
  2.0 0.0 copy-start.4
  2.0 0.0 copy-start.6
  2.0 0.0 copy-start.1
  2.1 0.0 copy-done
  2.1 0.5 %shard_map.121 = (f32[19,8,128]{2,1,0:T(8,128)S(1)}, f32[19,8,128]{2,1,0:T(8,128)S(1)}, f32[12,8,128]{2,1,0:T(8,128)S(1)}, f32[12,8,128]{2,1,0:T(8,128)S(1)}, f3...) custom-call(f32[2304,128]{1,0:T(8,128)S(1)} %bitcast.10, s32[128,128]{1,0:T(8,128)S(1)} %bitcast.12), custom_call_target="tpu_custom_call" | custom-call | flops 1000000 | bytes 1000000 | tf_op jit(solution)/shard_map/pallas_call | solution.py:751
  2.6 3.0 %collective-permute-start.2 = (f32[12,8,128]{2,1,0:T(8,128)S(1)}, f32[12,8,128]{2,1,0:T(8,128)S(1)}, u32[]{:S(2)}, u32[]{:S(2)}) collective-permute-start(f32[12,8,128]{2,1,0:T(8,128)S(1)} %get-tuple-element.31), channel_id=1, source_target_pairs={{0,1},{1,0},{2,3},{3,2},{4,5},{5,4},{6,7},{7,6},{8,9},{9,8},{10,11... | collective-permute-start | bytes 147464 | tf_op jit(solution)/shard_map/ppermute | solution.py:713
  5.6 2.6 %collective-permute-start.3 = (f32[12,8,128]{2,1,0:T(8,128)S(1)}, f32[12,8,128]{2,1,0:T(8,128)S(1)}, u32[]{:S(2)}, u32[]{:S(2)}) collective-permute-start(f32[12,8,128]{2,1,0:T(8,128)S(1)} %get-tuple-element.32), channel_id=1, source_target_pairs={{0,16},{1,2},{2,1},{3,19},{4,20},{5,6},{6,5},{7,23},{8,24},{9,10},... | collective-permute-start | bytes 147464 | tf_op jit(solution)/shard_map/ppermute | solution.py:713
  8.2 0.0 collective-permute-start
  8.2 1.5 %collective-permute-start.1 = (f32[19,8,128]{2,1,0:T(8,128)S(1)}, f32[19,8,128]{2,1,0:T(8,128)S(1)}, u32[]{:S(2)}, u32[]{:S(2)}) collective-permute-start(f32[19,8,128]{2,1,0:T(8,128)S(1)} %get-tuple-element.30), channel_id=1, source_target_pairs={{0,28},{4,8},{8,4},{12,16},{16,12},{20,24},{24,20},{28,0},{1,29},{... | collective-permute-start | bytes 233480 | tf_op jit(solution)/shard_map/ppermute | solution.py:701
  9.7 0.0 copy-done.7
  9.7 0.1 multiply_divide_fusion
  9.7 0.0 copy-done.5
  9.7 0.0 copy-done.4
  9.8 0.1 broadcast_multiply_fusion
  9.9 0.0 copy-done.6
  9.9 0.0 collective-permute-done.2.near_a
  9.9 0.8 %collective-permute-done.3.near_b = f32[12,8,128]{2,1,0:T(8,128)S(1)} collective-permute-done((f32[12,8,128]{2,1,0:T(8,128)S(1)}, f32[12,8,128]{2,1,0:T(8,128)S(1)}, u32[]{:S(2)}, u32[]{:S(2)}) %collective-permute-start.3) | collective-permute-done | bytes 49184 | tf_op jit(solution)/shard_map/ppermute | solution.py:713
  10.7 0.0 collective-permute-done.edge_a.id_edge_a
  10.7 3.2 %collective-permute-done.1.edge_b.id_edge_b = f32[19,8,128]{2,1,0:T(8,128)S(1)} collective-permute-done((f32[19,8,128]{2,1,0:T(8,128)S(1)}, f32[19,8,128]{2,1,0:T(8,128)S(1)}, u32[]{:S(2)}, u32[]{:S(2)}) %collective-permute-start.1) | collective-permute-done | bytes 77856 | tf_op jit(solution)/shard_map/ppermute | solution.py:701
  13.9 0.1 broadcast_in_dim.25.cv
  14.0 0.1 broadcast_in_dim.24.ap
  14.1 0.0 copy-done.1
  14.1 1.8 %shard_map.122 = (f32[12,24,8,256]{3,2,1,0:T(8,128)S(1)}, f32[6,16,8,256]{3,2,1,0:T(8,128)S(1)}, f32[16,8,256]{2,1,0:T(8,128)S(1)}, f32[16,8,128]{2,1,0:T(8,128)S(1)}, f32[42,8,128]{2,1,0:T(8,128)S(1)}) custom-call(f32[2304,128]{1,0:T(8,128)S(1)} %bitcast.11, s32[128,128]{1,0:T(8,128)S(1)} %bitcast.13, ...), custom_call_target="tpu_custom_call" | custom-call | flops 10000000 | bytes 10000000 | tf_op jit(solution)/shard_map/pallas_call | solution.py:778
  15.9 0.0 copy-start.2
  15.9 0.0 copy-start.3
  16.0 0.9 %shard_map.123 = (f32[6,16,8,256]{3,2,1,0:T(8,128)S(1)}, f32[42,8,128]{2,1,0:T(8,128)S(1)}) custom-call(f32[12,24,8,256]{3,2,1,0:T(8,128)S(1)} %get-tuple-element.35.stress.stress_in, f32[6,16,8,256]{3,2,1,0:T(8,128)S(1)} %get-tuple-element.36.vel_in, f32[16,8,256]{2,1,0:T(8,128)S(1)} %get-tuple-element.37.rho, f32[16,8,128]{2,1,0:T(8,128)S(1)} %get-tuple-element.38.id_side, ...), custom_call_target="tpu_custom_call" | custom-call | flops 10000000 | bytes 10000000 | tf_op jit(solution)/shard_map/pallas_call | solution.py:785
  16.8 0.7 %collective-permute-start.6 = (f32[42,8,128]{2,1,0:T(8,128)S(1)}, f32[42,8,128]{2,1,0:T(8,128)S(1)}, u32[]{:S(2)}, u32[]{:S(2)}) collective-permute-start(f32[42,8,128]{2,1,0:T(8,128)S(1)} %get-tuple-element.46), channel_id=1, source_target_pairs={{0,1},{1,0},{2,3},{3,2},{4,5},{5,4},{6,7},{7,6},{8,9},{9,8},{10,11... | collective-permute-start | bytes 516104 | tf_op jit(solution)/shard_map/ppermute | solution.py:713
  17.5 0.5 %collective-permute-start.7 = (f32[42,8,128]{2,1,0:T(8,128)S(1)}, f32[42,8,128]{2,1,0:T(8,128)S(1)}, u32[]{:S(2)}, u32[]{:S(2)}) collective-permute-start(f32[42,8,128]{2,1,0:T(8,128)S(1)} %get-tuple-element.47), channel_id=1, source_target_pairs={{0,16},{1,2},{2,1},{3,19},{4,20},{5,6},{6,5},{7,23},{8,24},{9,10},... | collective-permute-start | bytes 516104 | tf_op jit(solution)/shard_map/ppermute | solution.py:713
  18.0 2.4 %collective-permute-start.4 = (f32[28,8,128]{2,1,0:T(8,128)S(1)}, f32[28,8,128]{2,1,0:T(8,128)S(1)}, u32[]{:S(2)}, u32[]{:S(2)}) collective-permute-start(f32[28,8,128]{2,1,0:T(8,128)S(1)} %get-tuple-element.40), channel_id=1, source_target_pairs={{0,1},{1,0},{2,3},{3,2},{4,5},{5,4},{6,7},{7,6},{8,9},{9,8},{10,11... | collective-permute-start | bytes 344072 | tf_op jit(solution)/shard_map/ppermute | solution.py:713
  20.4 0.9 %collective-permute-start.5 = (f32[28,8,128]{2,1,0:T(8,128)S(1)}, f32[28,8,128]{2,1,0:T(8,128)S(1)}, u32[]{:S(2)}, u32[]{:S(2)}) collective-permute-start(f32[28,8,128]{2,1,0:T(8,128)S(1)} %get-tuple-element.41), channel_id=1, source_target_pairs={{0,16},{1,2},{2,1},{3,19},{4,20},{5,6},{6,5},{7,23},{8,24},{9,10},... | collective-permute-start | bytes 344072 | tf_op jit(solution)/shard_map/ppermute | solution.py:713
  21.3 1.5 %shard_map.124 = (f32[4,28,8,256]{3,2,1,0:T(8,128)S(1)}, f32[4,28,8,256]{3,2,1,0:T(8,128)S(1)}) custom-call(f32[10,512]{1,0:T(8,128)S(1)} %select_maximum_fusion.given), custom_call_target="tpu_custom_call" | custom-call | flops 100000000 | bytes 100000000 | tf_op jit(solution)/shard_map/pallas_call | solution.py:790
  22.8 6.3 %collective-permute-done.4.far_a = f32[28,8,128]{2,1,0:T(8,128)S(1)} collective-permute-done((f32[28,8,128]{2,1,0:T(8,128)S(1)}, f32[28,8,128]{2,1,0:T(8,128)S(1)}, u32[]{:S(2)}, u32[]{:S(2)}) %collective-permute-start.4) | collective-permute-done | bytes 114720 | tf_op jit(solution)/shard_map/ppermute | solution.py:713
  29.1 2.3 %collective-permute-done.5.far_b = f32[28,8,128]{2,1,0:T(8,128)S(1)} collective-permute-done((f32[28,8,128]{2,1,0:T(8,128)S(1)}, f32[28,8,128]{2,1,0:T(8,128)S(1)}, u32[]{:S(2)}, u32[]{:S(2)}) %collective-permute-start.5) | collective-permute-done | bytes 114720 | tf_op jit(solution)/shard_map/ppermute | solution.py:713
  31.4 0.0 copy-done.2
  31.4 0.0 copy-done.3
  31.4 2.0 %shard_map.125 = (f32[12,8,8,128]{3,2,1,0:T(8,128)S(1)}, f32[3,24,8,256]{3,2,1,0:T(8,128)S(1)}, f32[6,16,8,256]{3,2,1,0:T(8,128)S(1)}, f32[12,8,8,256]{3,2,1,0:T...) custom-call(f32[12,24,8,256]{3,2,1,0:T(8,128)S(1)} %get-tuple-element.35.stress.stress_in, ...), custom_call_target="tpu_custom_call" | custom-call | flops 100000000 | bytes 100000000 | tf_op jit(solution)/shard_map/pallas_call | solution.py:796
  33.4 0.0 collective-permute-done.6.got_a
  33.4 0.0 collective-permute-done.7.got_b
  33.5 4.7 %shard_map.126 = (f32[1152,128]{1,0:T(8,128)}, f32[1152,128]{1,0:T(8,128)}, f32[128,128]{1,0:T(8,128)}) custom-call(f32[6,16,8,256]{3,2,1,0:T(8,128)S(1)} %get-tuple-element.44.vel_in, f32[12,24,8,256]{3,2,1,0:T(8,128)S(1)} %get-tuple-element.35.stress.stress_in, f32[12,8,8,128]{3,2,1,0:T(8,128)S(1)} %get-tuple-element.45.halo, ...), custom_call_target="tpu_custom_call" | custom-call | flops 100000000 | bytes 100000000 | tf_op jit(solution)/shard_map/pallas_call | solution.py:814
  (6 shorter events, 0.0 us)
Async XLA Ops:
  0.6 1.4 %copy-start = (s32[8,16,128]{2,1,0:T(8,128)S(1)}, s32[8,16,128]{2,1,0:T(8,128)}, u32[]{:S(2)}) copy-start(s32[8,16,128]{2,1,0:T(8,128)} %param.12) | copy-start | bytes 196612
  2.0 7.7 %copy-start.7 = (s32[8]{0:T(128)S(1)}, s32[8]{0:T(128)}, u32[]{:S(2)}) copy-start(s32[8]{0:T(128)} %param.16) | copy-start | bytes 100
  2.0 7.7 %copy-start.5 = (s32[512]{0:T(512)S(1)}, s32[512]{0:T(512)}, u32[]{:S(2)}) copy-start(s32[512]{0:T(512)} %param.18) | copy-start | bytes 6148
  2.0 7.7 %copy-start.4 = (f32[2,3,512]{2,0,1:T(2,128)S(1)}, f32[2,3,512]{2,0,1:T(2,128)}, u32[]{:S(2)}) copy-start(f32[2,3,512]{2,0,1:T(2,128)} %param.19) | copy-start | bytes 36868
  2.0 7.8 %copy-start.6 = (f32[2,8]{1,0:T(2,128)S(1)}, f32[2,8]{1,0:T(2,128)}, u32[]{:S(2)}) copy-start(f32[2,8]{1,0:T(2,128)} %param.17) | copy-start | bytes 196
  2.0 12.0 %copy-start.1 = (f32[16]{0:T(128)S(1)}, f32[16]{0:T(128)}, u32[]{:S(2)}) copy-start(f32[16]{0:T(128)} %density_t.1) | copy-start | bytes 196
  2.6 7.3 %collective-permute-start.2 = (f32[12,8,128]{2,1,0:T(8,128)S(1)}, f32[12,8,128]{2,1,0:T(8,128)S(1)}, u32[]{:S(2)}, u32[]{:S(2)}) collective-permute-start(f32[12,8,128]{2,1,0:T(8,128)S(1)} %get-tuple-element.31), channel_id=1, source_target_pairs={{0,1},{1,0},{2,3},{3,2},{4,5},{5,4},{6,7},{7,6},{8,9},{9,8},{10,11... | collective-permute-start | bytes 147464 | tf_op jit(solution)/shard_map/ppermute | solution.py:713
  5.6 5.1 %collective-permute-start.3 = (f32[12,8,128]{2,1,0:T(8,128)S(1)}, f32[12,8,128]{2,1,0:T(8,128)S(1)}, u32[]{:S(2)}, u32[]{:S(2)}) collective-permute-start(f32[12,8,128]{2,1,0:T(8,128)S(1)} %get-tuple-element.32), channel_id=1, source_target_pairs={{0,16},{1,2},{2,1},{3,19},{4,20},{5,6},{6,5},{7,23},{8,24},{9,10},... | collective-permute-start | bytes 147464 | tf_op jit(solution)/shard_map/ppermute | solution.py:713
  8.2 2.5 %collective-permute-start = (f32[19,8,128]{2,1,0:T(8,128)S(1)}, f32[19,8,128]{2,1,0:T(8,128)S(1)}, u32[]{:S(2)}, u32[]{:S(2)}) collective-permute-start(f32[19,8,128]{2,1,0:T(8,128)S(1)} %get-tuple-element.29), channel_id=1, source_target_pairs={{0,4},{4,0},{8,12},{12,8},{16,20},{20,16},{24,28},{28,24},{1,5},{5... | collective-permute-start | bytes 233480 | tf_op jit(solution)/shard_map/ppermute | solution.py:701
  8.2 5.7 %collective-permute-start.1 = (f32[19,8,128]{2,1,0:T(8,128)S(1)}, f32[19,8,128]{2,1,0:T(8,128)S(1)}, u32[]{:S(2)}, u32[]{:S(2)}) collective-permute-start(f32[19,8,128]{2,1,0:T(8,128)S(1)} %get-tuple-element.30), channel_id=1, source_target_pairs={{0,28},{4,8},{8,4},{12,16},{16,12},{20,24},{24,20},{28,0},{1,29},{... | collective-permute-start | bytes 233480 | tf_op jit(solution)/shard_map/ppermute | solution.py:701
  15.9 15.5 %copy-start.2 = (f32[16]{0:T(128)S(1)}, f32[16]{0:T(128)}, u32[]{:S(2)}) copy-start(f32[16]{0:T(128)} %lame_t.1) | copy-start | bytes 196
  15.9 15.5 %copy-start.3 = (f32[16]{0:T(128)S(1)}, f32[16]{0:T(128)}, u32[]{:S(2)}) copy-start(f32[16]{0:T(128)} %shear_t.1) | copy-start | bytes 196
  16.8 16.6 %collective-permute-start.6 = (f32[42,8,128]{2,1,0:T(8,128)S(1)}, f32[42,8,128]{2,1,0:T(8,128)S(1)}, u32[]{:S(2)}, u32[]{:S(2)}) collective-permute-start(f32[42,8,128]{2,1,0:T(8,128)S(1)} %get-tuple-element.46), channel_id=1, source_target_pairs={{0,1},{1,0},{2,3},{3,2},{4,5},{5,4},{6,7},{7,6},{8,9},{9,8},{10,11... | collective-permute-start | bytes 516104 | tf_op jit(solution)/shard_map/ppermute | solution.py:713
  17.5 16.0 %collective-permute-start.7 = (f32[42,8,128]{2,1,0:T(8,128)S(1)}, f32[42,8,128]{2,1,0:T(8,128)S(1)}, u32[]{:S(2)}, u32[]{:S(2)}) collective-permute-start(f32[42,8,128]{2,1,0:T(8,128)S(1)} %get-tuple-element.47), channel_id=1, source_target_pairs={{0,16},{1,2},{2,1},{3,19},{4,20},{5,6},{6,5},{7,23},{8,24},{9,10},... | collective-permute-start | bytes 516104 | tf_op jit(solution)/shard_map/ppermute | solution.py:713
  18.0 11.2 %collective-permute-start.4 = (f32[28,8,128]{2,1,0:T(8,128)S(1)}, f32[28,8,128]{2,1,0:T(8,128)S(1)}, u32[]{:S(2)}, u32[]{:S(2)}) collective-permute-start(f32[28,8,128]{2,1,0:T(8,128)S(1)} %get-tuple-element.40), channel_id=1, source_target_pairs={{0,1},{1,0},{2,3},{3,2},{4,5},{5,4},{6,7},{7,6},{8,9},{9,8},{10,11... | collective-permute-start | bytes 344072 | tf_op jit(solution)/shard_map/ppermute | solution.py:713
  20.4 11.0 %collective-permute-start.5 = (f32[28,8,128]{2,1,0:T(8,128)S(1)}, f32[28,8,128]{2,1,0:T(8,128)S(1)}, u32[]{:S(2)}, u32[]{:S(2)}) collective-permute-start(f32[28,8,128]{2,1,0:T(8,128)S(1)} %get-tuple-element.41), channel_id=1, source_target_pairs={{0,16},{1,2},{2,1},{3,19},{4,20},{5,6},{6,5},{7,23},{8,24},{9,10},... | collective-permute-start | bytes 344072 | tf_op jit(solution)/shard_map/ppermute | solution.py:713
